TPU v7x, 8 devices: a whole 2x2x1 slice. The times are simulated.
8 devices in a mesh: dp: 1 (over z), tp: 8 (over y, x, core).
Axes of the slice: x: 2, y: 2, z: 1, core: 2. Of those that a mesh axis runs over, the one named last changes fastest.
Arguments:
- hidden: bfloat16 [3, 4096], P('dp')
- positions: int32 [3], P('dp')
- k_local: bfloat16 [3, 4096, 8, 128], P('dp', None, 'tp')
- v_local: bfloat16 [3, 4096, 8, 128], P('dp', None, 'tp')
- k_global: bfloat16 [3, 24576, 8, 128], P('dp', None, 'tp')
- v_global: bfloat16 [3, 24576, 8, 128], P('dp', None, 'tp')
- w_query: bfloat16 [2, 4096, 4096], P(None, None, 'tp')
- w_key: bfloat16 [2, 4096, 1024], P(None, None, 'tp')
- w_value: bfloat16 [2, 4096, 1024], P(None, None, 'tp')
- w_out: bfloat16 [2, 4096, 4096], P(None, 'tp')
- w_gate: bfloat16 [2, 4096, 14336], P(None, None, 'tp')
- w_up: bfloat16 [2, 4096, 14336], P(None, None, 'tp')
- w_down: bfloat16 [2, 14336, 4096], P(None, 'tp')
- norm_scale: float32 [2, 4, 4096], replicated
Outputs:
- output 1: bfloat16 [3, 4096], P('dp')
- output 2: bfloat16 [3, 4096, 8, 128], P('dp', None, 'tp')
- output 3: bfloat16 [3, 4096, 8, 128], P('dp', None, 'tp')
- output 4: bfloat16 [3, 24576, 8, 128], P('dp', None, 'tp')
- output 5: bfloat16 [3, 24576, 8, 128], P('dp', None, 'tp')
All inputs are finite; a program needn't handle non-finite values.
Results may differ from a plain program's by a relative error of at most 0.02.
Values are sent between devices in bfloat16 or wider.
A program may use at most 1 GiB of HBM per device.

v0:
```python
import jax
import jax.numpy as jnp
from jax import lax
from jax.sharding import PartitionSpec as P

SOFT_CAP = 50.0
NORM_EPS = 1e-6
ROPE_BASE = 10000.0
NEG_FILL = -1e30


def rms_norm(values, gain_row):
    values_f32 = values.astype(jnp.float32)
    inv_rms = lax.rsqrt(jnp.mean(values_f32 * values_f32, axis=-1, keepdims=True) + NORM_EPS)
    return (values_f32 * inv_rms * (1.0 + gain_row)).astype(jnp.bfloat16)


def rotary(projected, positions):
    head_dim = projected.shape[-1]
    half_dim = head_dim // 2
    inv_freq = ROPE_BASE ** (-2.0 * jnp.arange(half_dim, dtype=jnp.float32) / head_dim)
    angles = positions.astype(jnp.float32)[:, None, None] * inv_freq
    cos_part = jnp.cos(angles)
    sin_part = jnp.sin(angles)
    first_half = projected[..., :half_dim]
    second_half = projected[..., half_dim:]
    return jnp.concatenate([first_half * cos_part - second_half * sin_part, second_half * cos_part + first_half * sin_part], axis=-1)


def project_and_store(hidden, positions, k_cache, v_cache, slot_ids, w_query, w_key, w_value, gain_row):
    batch_rows = hidden.shape[0]
    kv_count = k_cache.shape[2]
    head_dim = k_cache.shape[3]
    normed = rms_norm(hidden, gain_row)
    queries = rotary(jnp.dot(normed, w_query, preferred_element_type=jnp.float32).reshape(batch_rows, -1, head_dim), positions)
    key_new = rotary(jnp.dot(normed, w_key, preferred_element_type=jnp.float32).reshape(batch_rows, kv_count, head_dim), positions)
    value_new = jnp.dot(normed, w_value, preferred_element_type=jnp.float32).reshape(batch_rows, kv_count, head_dim)
    slot_iota = lax.broadcasted_iota(jnp.int32, (batch_rows, k_cache.shape[1]), 1)
    slot_hit = (slot_iota == slot_ids[:, None])[:, :, None, None]
    k_cache = jnp.where(slot_hit, key_new.astype(jnp.bfloat16)[:, None], k_cache)
    v_cache = jnp.where(slot_hit, value_new.astype(jnp.bfloat16)[:, None], v_cache)
    grouped = queries.astype(jnp.bfloat16).reshape(batch_rows, kv_count, -1, head_dim)
    return grouped, k_cache, v_cache


def attention(grouped, k_cache, v_cache, key_valid):
    head_dim = grouped.shape[-1]
    logits = jnp.einsum('bgrd,bngd->bgrn', grouped, k_cache, preferred_element_type=jnp.float32) * head_dim ** -0.5
    logits = SOFT_CAP * jnp.tanh(logits / SOFT_CAP)
    if key_valid is not None:
        logits = jnp.where(key_valid[:, None, None, :], logits, NEG_FILL)
    attn_probs = jax.nn.softmax(logits, axis=-1).astype(jnp.bfloat16)
    mixed_heads = jnp.einsum('bgrn,bngd->bgrd', attn_probs, v_cache, preferred_element_type=jnp.float32)
    return mixed_heads.astype(jnp.bfloat16)


def mlp_part(normed, w_gate, w_up, w_down):
    gate_proj = jnp.dot(normed, w_gate, preferred_element_type=jnp.float32)
    up_proj = jnp.dot(normed, w_up, preferred_element_type=jnp.float32)
    hidden_act = (jax.nn.gelu(gate_proj, approximate=True) * up_proj).astype(jnp.bfloat16)
    return jnp.dot(hidden_act, w_down, preferred_element_type=jnp.float32)


def add_normed(hidden, branch_sum, gain_row):
    return (hidden.astype(jnp.float32) + rms_norm(branch_sum, gain_row).astype(jnp.float32)).astype(jnp.bfloat16)


def decoder_layer(hidden, positions, k_cache, v_cache, slot_ids, key_valid, layer_weights, gains):
    w_query, w_key, w_value, w_out, w_gate, w_up, w_down = layer_weights
    grouped, k_cache, v_cache = project_and_store(hidden, positions, k_cache, v_cache, slot_ids, w_query, w_key, w_value, gains[0])
    mixed_heads = attention(grouped, k_cache, v_cache, key_valid)
    attn_part = jnp.dot(mixed_heads.reshape(hidden.shape[0], -1), w_out, preferred_element_type=jnp.float32)
    attn_sum = lax.psum(attn_part.astype(jnp.bfloat16), 'tp')
    hidden = add_normed(hidden, attn_sum, gains[1])
    down_part = mlp_part(rms_norm(hidden, gains[2]), w_gate, w_up, w_down)
    down_sum = lax.psum(down_part.astype(jnp.bfloat16), 'tp')
    hidden = add_normed(hidden, down_sum, gains[3])
    return hidden, k_cache, v_cache


def decode_step(hidden, positions, k_local, v_local, k_global, v_global, w_query, w_key, w_value, w_out, w_gate, w_up, w_down, norm_scale):
    stacks = (w_query, w_key, w_value, w_out, w_gate, w_up, w_down)
    window = k_local.shape[1]
    global_valid = lax.broadcasted_iota(jnp.int32, (hidden.shape[0], k_global.shape[1]), 1) <= positions[:, None]
    hidden, k_local, v_local = decoder_layer(hidden, positions, k_local, v_local, positions % window, None, tuple(stacked[0] for stacked in stacks), norm_scale[0])
    hidden, k_global, v_global = decoder_layer(hidden, positions, k_global, v_global, positions, global_valid, tuple(stacked[1] for stacked in stacks), norm_scale[1])
    return hidden, k_local, v_local, k_global, v_global


def solution(mesh):
    row_spec = P('dp', None)
    cache_spec = P('dp', None, 'tp', None)
    col_split = P(None, None, 'tp')
    row_split = P(None, 'tp', None)
    in_specs = (row_spec, P('dp'), cache_spec, cache_spec, cache_spec, cache_spec, col_split, col_split, col_split, row_split, col_split, col_split, row_split, P())
    out_specs = (row_spec, cache_spec, cache_spec, cache_spec, cache_spec)
    return jax.shard_map(decode_step, mesh=mesh, in_specs=in_specs, out_specs=out_specs, check_vma=False)
```

profile of v0, /device:TPU:0, one launch (start us, length us, event | category | flops | bytes accessed | tf_op | source)
XLA Modules:
  0.0 234.6 jit_solution(13219702265419666039)
XLA Ops:
  0.7 0.9 fusion.94
  1.6 0.7 fusion.174
  2.3 0.1 multiply_cosine_fusion.1
  2.4 0.1 iota_compare_fusion.2
  2.6 2.0 slice_add_fusion
  4.5 1.5 convolution_convert_fusion.3
  6.1 1.6 convolution_bitcast_fusion.1
  7.6 0.1 fusion.157
  7.8 0.1 pad_maximum_fusion.2
  7.8 1.0 iota_compare_fusion.1
  8.8 8.0 %broadcast_select_fusion.3 = (bf16[3,4096,1,128]{3,1,2,0:T(8,128)(2,1)S(1)}, bf16[3,4096,1,128]{3,1,2,0:T(8,128)(2,1)}) fusion(bf16[3,4096,1,128]{3,1,2,0:T(8,128)(2,1)} %param.16, pred[3,4096]{1,0:T(4,128)(4,1)S(1)} %iota_compare_fusion.2, bf16[3,128]{1,0:T(4,128)(2,1)S(1)} %pad_maximum_fusion.2, bf16[3,4096,1,128]{3,1,2,0:T(8,128)(2,1)} %param.17, ...), kind=kLoop, calls=%fused_computation.47 | loop fusion | flops 3145728 | bytes 12596736 | tf_op jit(solution)/shard_map/jit(_where)/select_n | solution.py:40
  16.8 3.8 %slice_bitcast_fusion = (bf16[512,4096]{0,1:T(8,128)(2,1)}, bf16[512,4096]{0,1:T(8,128)(2,1)}) fusion(bf16[2,4096,512]{2,1,0:T(8,128)(2,1)S(1)} %bitcast.133), kind=kLoop, calls=%fused_computation.40 | loop fusion | bytes 16777216 | tf_op jit(solution)/shard_map/dot_general | solution.py:35
  20.6 6.4 %copy.21 = bf16[512,4096]{1,0:T(8,128)(2,1)} copy(bf16[512,4096]{0,1:T(8,128)(2,1)} %get-tuple-element.11) | data formatting | bytes 8388608 | tf_op jit(solution)/shard_map/dot_general | solution.py:35
  27.0 6.3 %copy.19 = bf16[512,4096]{1,0:T(8,128)(2,1)} copy(bf16[512,4096]{0,1:T(8,128)(2,1)} %get-tuple-element.12) | data formatting | bytes 8388608 | tf_op jit(solution)/shard_map/dot_general | solution.py:35
  33.4 3.4 %fusion.112 = f32[3,4,128]{2,0,1:T(4,128)S(1)} fusion(bf16[4,128,4096]{2,1,0:T(8,128)(2,1)} %bitcast.129, bf16[3,4096]{1,0:T(4,128)(2,1)S(1)} %copy-done.1, f32[4096]{0:T(1024)S(1)} %bitcast.143, f32[3]{0:T(128)S(1)} %add_rsqrt_fusion.7), kind=kOutput, calls=%fused_computation.130 | convolution fusion | flops 12632064 | bytes 4241420 | tf_op jit(solution)/shard_map/dot_general | solution.py:35
  36.7 0.1 subtract_convert_fusion.1
  36.8 0.7 pad_maximum_fusion
  37.5 2.4 %fusion.175 = (f32[3,4]{1,0:T(4,128)}, f32[3,4,4096]{2,1,0:T(4,128)S(1)}) fusion(bf16[3,4096,1,128]{3,1,2,0:T(8,128)(2,1)S(1)} %get-tuple-element.23, bf16[3,4,128]{2,0,1:T(4,128)(2,1)} %pad_maximum_fusion), kind=kOutput, calls=%fused_computation.206 | convolution fusion | flops 12783615 | bytes 3345456 | tf_op jit(solution)/shard_map/sub | solution.py:52
  39.9 2.5 %fusion.63 = bf16[1,3,4,128]{3,2,1,0:T(4,128)(2,1)S(1)} fusion(bf16[3,4096,1,128]{3,1,2,0:T(8,128)(2,1)} %get-tuple-element.24, f32[3,4,4096]{2,1,0:T(4,128)S(1)} %get-tuple-element.40, f32[3,4]{1,0:T(4,128)} %get-tuple-element.39), kind=kOutput, calls=%fused_computation.57 | convolution fusion | flops 12682752 | bytes 3345456 | tf_op jit(solution)/shard_map/bgrn,bngd->bgrd/dot_general | solution.py:53
  42.4 2.9 %convolution_convert_fusion.1 = bf16[3,4096]{1,0:T(4,128)(2,1)S(1)} fusion(bf16[2,512,4096]{2,1,0:T(8,128)(2,1)} %param.23, bf16[1,3,4,128]{3,2,1,0:T(4,128)(2,1)S(1)} %fusion.63), kind=kOutput, calls=%fused_computation.36 | convolution fusion | flops 12595200 | bytes 4221952 | tf_op jit(solution)/shard_map/dot_general | solution.py:72
  45.2 25.2 %psum.28 = bf16[3,4096]{1,0:T(4,128)(2,1)S(1)} all-reduce(bf16[3,4096]{1,0:T(4,128)(2,1)S(1)} %convolution_convert_fusion.1), channel_id=1, replica_groups=mesh['dp'=1,'tp'=8] {'tp'}, use_global_device_ids=true, to_apply=%region_3.4 | all-reduce | flops 12288 | bytes 49152 | tf_op jit(solution)/shard_map/psum | solution.py:73
  70.5 0.1 fusion.82
  70.6 0.2 fusion.98
  70.9 6.3 %fusion.120 = f32[3,1792]{1,0:T(4,128)S(1)} fusion(bf16[2,4096,1792]{2,1,0:T(8,128)(2,1)} %param.24, bf16[3,4096]{1,0:T(4,128)(2,1)S(1)} %get-tuple-element.10, f32[4096]{0:T(1024)S(1)} %bitcast.136, f32[3]{0:T(128)S(1)} %add_rsqrt_fusion.5), kind=kOutput, calls=%fused_computation.138 | convolution fusion | flops 44132352 | bytes 14742540 | tf_op jit(solution)/shard_map/dot_general | solution.py:58
  77.2 11.7 %fusion.29 = bf16[3,4096]{1,0:T(4,128)(2,1)S(1)} fusion(bf16[2,1792,4096]{2,1,0:T(8,128)(2,1)} %param.26, f32[3,1792]{1,0:T(4,128)S(1)} %fusion.120, bf16[2,4096,1792]{2,1,0:T(8,128)(2,1)} %param.25, bf16[3,4096]{1,0:T(4,128)(2,1)S(1)} %get-tuple-element.10, f32[4096]{0:T(1024)S(1)} %bitcast.137, f32[3]{0:T(128)S(1)} %add_rsqrt_fusion.5), kind=kOutput, calls=%fused_computation.33 | convolution fusion | flops 88152576 | bytes 29447180 | tf_op jit(solution)/shard_map/dot_general | solution.py:61
  89.0 23.4 %psum.29 = bf16[3,4096]{1,0:T(4,128)(2,1)S(1)} all-reduce(bf16[3,4096]{1,0:T(4,128)(2,1)S(1)} %fusion.29), channel_id=1, replica_groups=mesh['dp'=1,'tp'=8] {'tp'}, use_global_device_ids=true, to_apply=%region_6.7 | all-reduce | flops 12288 | bytes 49152 | tf_op jit(solution)/shard_map/psum | solution.py:76
  112.4 0.1 fusion.85
  112.5 0.2 fusion.102
  112.8 3.6 %fusion.110 = f32[3,4,128]{2,0,1:T(4,128)S(1)} fusion(bf16[4,128,4096]{2,1,0:T(8,128)(2,1)} %bitcast.128, bf16[3,4096]{1,0:T(4,128)(2,1)S(1)} %get-tuple-element.8, f32[4096]{0:T(1024)S(1)} %bitcast.138, f32[3]{0:T(128)S(1)} %add_rsqrt_fusion.3), kind=kOutput, calls=%fused_computation.128 | convolution fusion | flops 12632064 | bytes 4241420 | tf_op jit(solution)/shard_map/dot_general | solution.py:35
  116.3 0.1 subtract_convert_fusion
  116.4 0.1 pad_maximum_fusion.1
  116.5 0.3 convolution_convert_fusion.2
  116.8 0.3 convolution_bitcast_fusion
  117.1 0.1 fusion.155
  117.3 0.1 pad_maximum_fusion.3
  117.3 32.3 %broadcast_select_fusion.1 = (bf16[3,24576,1,128]{3,1,2,0:T(8,128)(2,1)}, bf16[3,24576,1,128]{3,1,2,0:T(8,128)(2,1)}) fusion(bf16[3,24576,1,128]{3,1,2,0:T(8,128)(2,1)} %param.18, pred[3,24576]{1,0:T(4,128)(4,1)S(1)} %get-tuple-element.36, bf16[3,128]{1,0:T(4,128)(2,1)S(1)} %pad_maximum_fusion.3, bf16[3,24576,1,128]{3,1,2,0:T(8,128)(2,1)} %param.19, ...), kind=kLoop, calls=%fused_computation.9 | loop fusion | flops 18874368 | bytes 75572736 | tf_op jit(solution)/shard_map/jit(_where)/select_n | solution.py:40
  149.6 9.2 %fusion.176 = (f32[3,4]{1,0:T(4,128)S(1)}, f32[3,4,24576]{2,1,0:T(4,128)S(1)}) fusion(bf16[3,24576,1,128]{3,1,2,0:T(8,128)(2,1)} %get-tuple-element.21, bf16[3,4,128]{2,0,1:T(4,128)(2,1)S(1)} %pad_maximum_fusion.1, pred[3,24576]{1,0:T(4,128)(4,1)S(1)} %get-tuple-element.35), kind=kOutput, calls=%fused_computation.207 | convolution fusion | flops 76677104 | bytes 20130864 | tf_op jit(solution)/shard_map/bgrd,bngd->bgrn/dot_general | solution.py:48
  158.8 0.6 fusion.74
  159.4 7.9 %fusion.60 = bf16[1,3,4,128]{3,2,1,0:T(4,128)(2,1)S(1)} fusion(bf16[3,24576,1,128]{3,1,2,0:T(8,128)(2,1)} %get-tuple-element.22, f32[3,4,24576]{2,1,0:T(4,128)S(1)} %get-tuple-element.42, f32[3,4]{1,0:T(4,128)S(1)} %fusion.74, f32[3,4]{1,0:T(4,128)S(1)} %get-tuple-element.41), kind=kOutput, calls=%fused_computation.56 | convolution fusion | flops 76383744 | bytes 20057184 | tf_op jit(solution)/shard_map/bgrn,bngd->bgrd/dot_general | solution.py:53
  167.3 0.7 convolution_convert_fusion
  168.0 24.1 %psum.30 = bf16[3,4096]{1,0:T(4,128)(2,1)S(1)} all-reduce(bf16[3,4096]{1,0:T(4,128)(2,1)S(1)} %convolution_convert_fusion), channel_id=1, replica_groups=mesh['dp'=1,'tp'=8] {'tp'}, use_global_device_ids=true, to_apply=%region_11.12 | all-reduce | flops 12288 | bytes 49152 | tf_op jit(solution)/shard_map/psum | solution.py:73
  192.1 0.1 fusion.88
  192.3 0.2 fusion.106
  192.5 6.3 %fusion.129 = f32[3,1792]{1,0:T(4,128)S(1)} fusion(bf16[2,4096,1792]{2,1,0:T(8,128)(2,1)} %param.24, bf16[3,4096]{1,0:T(4,128)(2,1)S(1)} %get-tuple-element.6, f32[4096]{0:T(1024)S(1)} %bitcast.134, f32[3]{0:T(128)S(1)} %add_rsqrt_fusion.1), kind=kOutput, calls=%fused_computation.145 | convolution fusion | flops 44132352 | bytes 14742540 | tf_op jit(solution)/shard_map/dot_general | solution.py:58
  198.8 11.7 %fusion.32 = bf16[3,4096]{1,0:T(4,128)(2,1)S(1)} fusion(bf16[2,1792,4096]{2,1,0:T(8,128)(2,1)} %param.26, f32[3,1792]{1,0:T(4,128)S(1)} %fusion.129, bf16[2,4096,1792]{2,1,0:T(8,128)(2,1)} %param.25, bf16[3,4096]{1,0:T(4,128)(2,1)S(1)} %get-tuple-element.6, f32[4096]{0:T(1024)S(1)} %bitcast.135, f32[3]{0:T(128)S(1)} %add_rsqrt_fusion.1), kind=kOutput, calls=%fused_computation.34 | convolution fusion | flops 88152576 | bytes 29447180 | tf_op jit(solution)/shard_map/dot_general | solution.py:61
  210.6 23.2 %psum.31 = bf16[3,4096]{1,0:T(4,128)(2,1)S(1)} all-reduce(bf16[3,4096]{1,0:T(4,128)(2,1)S(1)} %fusion.32), channel_id=1, replica_groups=mesh['dp'=1,'tp'=8] {'tp'}, use_global_device_ids=true, to_apply=%region_14.15 | all-reduce | flops 12288 | bytes 49152 | tf_op jit(solution)/shard_map/psum | solution.py:76
  233.7 0.1 fusion.91
  233.9 0.7 fusion.109
  (57 shorter events, 0.2 us)
Async XLA Ops:
  0.6 16.1 %copy-start.13 = (f32[64]{0:T(128)}, f32[64]{0:T(128)S(1)}, u32[]{:S(2)}) copy-start(f32[64]{0:T(128)S(1)} %multiply_power_fusion) | copy-start | bytes 772
  2.3 14.5 %copy-start.15 = (f32[3]{0:T(128)}, f32[3]{0:T(128)S(1)}, u32[]{:S(2)}) copy-start(f32[3]{0:T(128)S(1)} %get-tuple-element.37) | copy-start | bytes 40
  2.4 34.3 %copy-start.9 = (f32[3,64]{1,0:T(4,128)}, f32[3,64]{1,0:T(4,128)S(1)}, u32[]{:S(2)}) copy-start(f32[3,64]{1,0:T(4,128)S(1)} %get-tuple-element.33) | copy-start | bytes 2308
  2.4 34.3 %copy-start.11 = (f32[3,64]{1,0:T(4,128)}, f32[3,64]{1,0:T(4,128)S(1)}, u32[]{:S(2)}) copy-start(f32[3,64]{1,0:T(4,128)S(1)} %get-tuple-element.34) | copy-start | bytes 2308
  2.5 14.2 %slice-start.2 = ((s8[8388608]{0:T(1024)(128)(4,1)}), s8[4194304]{0:T(1024)(128)(4,1)S(1)}, s32[]{:S(2)}) async-start(s8[8388608]{0:T(1024)(128)(4,1)} %bitcast.132), calls=%async_computation.2 | async-start | bytes 8388608
  8.8 8.0 %slice-start.3 = ((s8[8388608]{0:T(1024)(128)(4,1)}), s8[4194304]{0:T(1024)(128)(4,1)S(1)}, s32[]{:S(2)}) async-start(s8[8388608]{0:T(1024)(128)(4,1)} %bitcast.132), calls=%async_computation.3 | async-start | bytes 8388608
  16.8 20.7 %copy-start = (bf16[3,4096,1,128]{3,1,2,0:T(8,128)(2,1)}, bf16[3,4096,1,128]{3,1,2,0:T(8,128)(2,1)S(1)}, u32[]{:S(2)}) copy-start(bf16[3,4096,1,128]{3,1,2,0:T(8,128)(2,1)S(1)} %get-tuple-element.23) | copy-start | bytes 9437188
  27.0 6.3 %copy-start.1 = (bf16[3,4096]{1,0:T(4,128)(2,1)S(1)}, bf16[3,4096]{1,0:T(4,128)(2,1)}, u32[]{:S(2)}) copy-start(bf16[3,4096]{1,0:T(4,128)(2,1)} %param.14) | copy-start | bytes 73732
  39.9 30.7 %copy-start.2 = (bf16[3,4096]{1,0:T(4,128)(2,1)S(1)}, bf16[3,4096]{1,0:T(4,128)(2,1)}, u32[]{:S(2)}) copy-start(bf16[3,4096]{1,0:T(4,128)(2,1)} %param.14) | copy-start | bytes 73732
  39.9 30.7 %copy-start.8 = (f32[1,1,4096]{2,1,0:T(1,128)S(1)}, f32[1,1,4096]{2,1,0:T(1,128)}, u32[]{:S(2)}) copy-start(f32[1,1,4096]{2,1,0:T(1,128)} %get-tuple-element.18) | copy-start | bytes 49156
  39.9 30.9 %copy-start.3 = (f32[1,1,4096]{2,1,0:T(1,128)S(1)}, f32[1,1,4096]{2,1,0:T(1,128)}, u32[]{:S(2)}) copy-start(f32[1,1,4096]{2,1,0:T(1,128)} %get-tuple-element.17) | copy-start | bytes 49156
  77.2 35.3 %copy-start.7 = (f32[1,1,4096]{2,1,0:T(1,128)S(1)}, f32[1,1,4096]{2,1,0:T(1,128)}, u32[]{:S(2)}) copy-start(f32[1,1,4096]{2,1,0:T(1,128)} %get-tuple-element.16) | copy-start | bytes 49156
  77.2 35.6 %copy-start.4 = (f32[1,1,4096]{2,1,0:T(1,128)S(1)}, f32[1,1,4096]{2,1,0:T(1,128)}, u32[]{:S(2)}) copy-start(f32[1,1,4096]{2,1,0:T(1,128)} %get-tuple-element.15) | copy-start | bytes 49156
  88.9 27.4 %copy-start.10 = (f32[3,64]{1,0:T(4,128)S(1)}, f32[3,64]{1,0:T(4,128)}, u32[]{:S(2)}) copy-start(f32[3,64]{1,0:T(4,128)} %copy-done.9) | copy-start | bytes 2308
  88.9 27.4 %copy-start.12 = (f32[3,64]{1,0:T(4,128)S(1)}, f32[3,64]{1,0:T(4,128)}, u32[]{:S(2)}) copy-start(f32[3,64]{1,0:T(4,128)} %copy-done.11) | copy-start | bytes 2308
  88.9 27.6 %copy-start.17 = (bf16[2,4096,128]{2,1,0:T(8,128)(2,1)S(1)}, bf16[2,4096,128]{2,1,0:T(8,128)(2,1)}, u32[]{:S(2)}) copy-start(bf16[2,4096,128]{2,1,0:T(8,128)(2,1)} %param.22) | copy-start | bytes 6291460
  88.9 28.2 %copy-start.14 = (f32[64]{0:T(128)S(1)}, f32[64]{0:T(128)}, u32[]{:S(2)}) copy-start(f32[64]{0:T(128)} %copy-done.13) | copy-start | bytes 772
  88.9 28.2 %copy-start.16 = (f32[3]{0:T(128)S(1)}, f32[3]{0:T(128)}, u32[]{:S(2)}) copy-start(f32[3]{0:T(128)} %copy-done.15) | copy-start | bytes 40
  112.3 4.5 %copy-start.18 = (bf16[2,4096,128]{2,1,0:T(8,128)(2,1)S(1)}, bf16[2,4096,128]{2,1,0:T(8,128)(2,1)}, u32[]{:S(2)}) copy-start(bf16[2,4096,128]{2,1,0:T(8,128)(2,1)} %param.21) | copy-start | bytes 6291460
  149.6 17.7 %slice-start = ((s8[8388608]{0:T(1024)(128)(4,1)}), s8[4194304]{0:T(1024)(128)(4,1)S(1)}, s32[]{:S(2)}) async-start(s8[8388608]{0:T(1024)(128)(4,1)} %bitcast.130), calls=%async_computation | async-start | bytes 8388608
  159.4 7.9 %slice-start.1 = ((s8[8388608]{0:T(1024)(128)(4,1)}), s8[4194304]{0:T(1024)(128)(4,1)S(1)}, s32[]{:S(2)}) async-start(s8[8388608]{0:T(1024)(128)(4,1)} %bitcast.130), calls=%async_computation.1 | async-start | bytes 8388608
  167.3 24.9 %copy-start.6 = (f32[1,1,4096]{2,1,0:T(1,128)S(1)}, f32[1,1,4096]{2,1,0:T(1,128)}, u32[]{:S(2)}) copy-start(f32[1,1,4096]{2,1,0:T(1,128)} %get-tuple-element.14) | copy-start | bytes 49156
  198.8 35.1 %copy-start.5 = (f32[1,1,4096]{2,1,0:T(1,128)S(1)}, f32[1,1,4096]{2,1,0:T(1,128)}, u32[]{:S(2)}) copy-start(f32[1,1,4096]{2,1,0:T(1,128)} %get-tuple-element.13) | copy-start | bytes 49156
where the time goes:
time: 236 us; the launch traced here: 235 us
  blocking collectives  95.9 us (41%)
  matrix products  72.1 us (31%)
  other arithmetic  49 us (21%)
  local copies, waits for them, and re-layouts  16.7 us (7%)
    psum x2, blocking collectives, decoder_layer(): attn_sum = lax.psum(attn_part.astype(jnp.bfloat16), 'tp')  49.3 us
    psum x2, blocking collectives, decoder_layer(): down_sum = lax.psum(down_part.astype(jnp.bfloat16), 'tp')  46.5 us
    select_n x2, other arithmetic, project_and_store(): jnp.where(slot_hit, key_new.astype(jnp.bfloat16)[:, None], k_cache)  40.2 us
    dot_general x2, matrix products, mlp_part(): return jnp.dot(hidden_act, w_down, preferred_element_type=jnp.float32)  23.4 us
    dot_general x3, local copies, waits for them, and re-layouts, project_and_store(): jnp.dot(normed, w_query, preferred_element_type=jnp.float32)  16.6 us
    dot_general x2, matrix products, mlp_part(): gate_proj = jnp.dot(normed, w_gate, preferred_element_type=jnp.float32)  12.6 us
    dot_general x2, matrix products, attention(): jnp.einsum('bgrn,bngd->bgrd', attn_probs, v_cache, preferred_element_type...  10.4 us
    dot_general x1, matrix products, attention(): jnp.einsum('bgrd,bngd->bgrn', grouped, k_cache, preferred_element_type=jn...  9.16 us

commit v1 on v0

v1 whole, which is shorter than its diff:
```python
import functools

import jax
import jax.numpy as jnp
import numpy as np
from jax import lax
from jax.experimental import pallas as pl
from jax.experimental.pallas import tpu as pltpu
from jax.sharding import PartitionSpec as P

SOFT_CAP = 50.0
NORM_EPS = 1e-6
ROPE_BASE = 10000.0
HEAD = 128
MIB = 1024 * 1024
F32 = jnp.float32
BF16 = jnp.bfloat16


def norm_rows(values, gain_row):
    inv_rms = lax.rsqrt(jnp.mean(values * values, axis=-1, keepdims=True) + NORM_EPS)
    return (values * inv_rms * (1.0 + gain_row)).astype(BF16)


def matmul(lhs, rhs):
    return jnp.dot(lhs, rhs, preferred_element_type=F32)


def rotate(head, cos_part, sin_part):
    return head * cos_part + pltpu.roll(head, HEAD // 2, 1) * sin_part


def attn_kernel(layer, block, ahead, window, pos_ref, freq_ref, x_ref, gain_ref, wq_hbm, wk_hbm, wv_hbm, wo_hbm, k_hbm, v_hbm,
                o_ref, k_out, v_out, kbuf, vbuf, wq, wk, wv, wo, xbuf, ebuf, w_sem, kin_sem, vin_sem, kout_sem, vout_sem):
    batch, length = k_hbm.shape[0], k_hbm.shape[1]
    heads = wq.shape[1] // HEAD
    blocks = length // block

    def k_in(i):
        rows = pl.ds(i * block, block)
        return pltpu.make_async_copy(k_hbm.at[:, rows, :], kbuf.at[:, rows, :], kin_sem.at[i])

    def v_in(i):
        rows = pl.ds(i * block, block)
        return pltpu.make_async_copy(v_hbm.at[:, rows, :], vbuf.at[:, rows, :], vin_sem.at[i])

    def k_back(i):
        rows = pl.ds(i * block, block)
        return pltpu.make_async_copy(kbuf.at[:, rows, :], k_out.at[:, rows, :], kout_sem.at[i])

    def v_back(i):
        rows = pl.ds(i * block, block)
        return pltpu.make_async_copy(vbuf.at[:, rows, :], v_out.at[:, rows, :], vout_sem.at[i])

    wq_copy = pltpu.make_async_copy(wq_hbm.at[layer], wq, w_sem.at[0])
    wk_copy = pltpu.make_async_copy(wk_hbm.at[layer], wk, w_sem.at[1])
    wv_copy = pltpu.make_async_copy(wv_hbm.at[layer], wv, w_sem.at[2])
    wo_copy = pltpu.make_async_copy(wo_hbm.at[layer], wo, w_sem.at[3])
    wk_copy.start()
    wv_copy.start()
    wq_copy.start()
    for i in range(min(ahead, blocks)):
        k_in(i).start()

    xbuf[...] = jnp.zeros_like(xbuf)
    xbuf[0:batch, :] = x_ref[...].astype(F32)
    normed = norm_rows(xbuf[...], gain_ref[layer, 0:1, :])

    row_id = lax.broadcasted_iota(jnp.int32, (8, HEAD), 0)
    pos_rows = jnp.full((8, HEAD), pos_ref[0], jnp.int32)
    for b in range(1, batch):
        pos_rows = jnp.where(row_id == b, pos_ref[b], pos_rows)
    angles = pos_rows.astype(F32) * freq_ref[...]
    lane_id = lax.broadcasted_iota(jnp.int32, (8, HEAD), 1)
    cos_part = jnp.cos(angles)
    sin_part = jnp.sin(angles)
    sin_part = jnp.where(lane_id < HEAD // 2, -sin_part, sin_part)

    wk_copy.wait()
    key_new = rotate(matmul(normed, wk[...]), cos_part, sin_part).astype(BF16)
    wv_copy.wait()
    value_new = matmul(normed, wv[...]).astype(BF16)
    wq_copy.wait()
    queries = matmul(normed, wq[...])
    stacked = jnp.concatenate([rotate(queries[:, h * HEAD:(h + 1) * HEAD], cos_part, sin_part)[0:4] for h in range(heads)], axis=0)
    rows = 4 * heads
    of_row = lax.broadcasted_iota(jnp.int32, (rows, HEAD), 0) % 4
    lhs = jnp.concatenate([jnp.where(of_row == b, stacked, 0.0) for b in range(batch)], axis=1).astype(BF16)

    slots = [pos_ref[b] % window if window else pos_ref[b] for b in range(batch)]
    tile_rows = lax.broadcasted_iota(jnp.int32, (16, HEAD), 0)

    def put_row(buf, new_rows, i):
        for b in range(batch):
            @pl.when(slots[b] // block == i)
            def _():
                base = pl.multiple_of((slots[b] // 16) * 16, 16)
                tile = buf[b, pl.ds(base, 16), :]
                new_row = jnp.broadcast_to(new_rows[b:b + 1, :].astype(F32), (16, HEAD))
                kept = tile.astype(F32)
                buf[b, pl.ds(base, 16), :] = jnp.where(tile_rows == slots[b] - base, new_row, kept).astype(BF16)

    col_ids = lax.broadcasted_iota(jnp.int32, (rows, block), 1)
    of_col = lax.broadcasted_iota(jnp.int32, (rows, block), 0) % 4
    limits = jnp.full((rows, block), pos_ref[0], jnp.int32)
    for b in range(1, batch):
        limits = jnp.where(of_col == b, pos_ref[b], limits)

    def score_step(i, total):
        k_in(i).wait()

        @pl.when(i + ahead < blocks)
        def _():
            k_in(i + ahead).start()

        @pl.when(i + ahead >= blocks)
        def _():
            v_in(i + ahead - blocks).start()

        @pl.when(i == max(blocks - ahead, 0))
        def _():
            wo_copy.start()

        put_row(kbuf, key_new, i)
        span = pl.ds(i * block, block)
        keys = jnp.concatenate([kbuf[b, span, :] for b in range(batch)], axis=1)
        logits = lax.dot_general(lhs, keys, (((1,), (1,)), ((), ())), preferred_element_type=F32) * HEAD ** -0.5
        weights = jnp.exp(SOFT_CAP * jnp.tanh(logits / SOFT_CAP))
        if not window:
            weights = jnp.where(col_ids + i * block <= limits, weights, 0.0)
        ebuf[i] = weights
        k_back(i).start()
        return total + jnp.sum(weights, axis=-1, keepdims=True)

    total = lax.fori_loop(0, blocks, score_step, jnp.zeros((rows, 1), F32))
    inv_total = 1.0 / total

    def value_step(i, acc):
        v_in(i).wait()

        @pl.when(i + ahead < blocks)
        def _():
            v_in(i + ahead).start()

        put_row(vbuf, value_new, i)
        span = pl.ds(i * block, block)
        values = jnp.concatenate([vbuf[b, span, :] for b in range(batch)], axis=1)
        probs = (ebuf[i] * inv_total).astype(BF16)
        out = acc + matmul(probs, values)
        v_back(i).start()
        return out

    mixed = lax.fori_loop(0, blocks, value_step, jnp.zeros((rows, batch * HEAD), F32))
    picked = jnp.zeros((rows, HEAD), F32)
    for b in range(batch):
        picked = jnp.where(of_row == b, mixed[:, b * HEAD:(b + 1) * HEAD], picked)
    merged = jnp.concatenate([picked[4 * h:4 * h + 4, :] for h in range(heads)], axis=1).astype(BF16)
    wo_copy.wait()
    o_ref[...] = matmul(merged, wo[...]).astype(BF16)

    def drain(i, carry):
        k_back(i).wait()
        v_back(i).wait()
        return carry

    lax.fori_loop(0, blocks, drain, 0)


def attn_call(layer, block, ahead, window, positions, freqs, hidden, gains, w_query, w_key, w_value, w_out, k_cache, v_cache):
    batch, length, head = k_cache.shape
    width, q_cols = w_query.shape[1:]
    blocks = length // block
    vmem = pl.BlockSpec(memory_space=pltpu.VMEM)
    hbm = pl.BlockSpec(memory_space=pl.ANY)
    smem = pl.BlockSpec(memory_space=pltpu.SMEM)
    cache = jax.ShapeDtypeStruct(k_cache.shape, k_cache.dtype)
    return pl.pallas_call(
        functools.partial(attn_kernel, layer, block, ahead, window),
        name=f"attn{layer}",
        out_shape=(jax.ShapeDtypeStruct((4, width), BF16), cache, cache),
        in_specs=[smem, vmem, vmem, vmem] + [hbm] * 6,
        out_specs=(vmem, hbm, hbm),
        scratch_shapes=[
            pltpu.VMEM(k_cache.shape, BF16),
            pltpu.VMEM(k_cache.shape, BF16),
            pltpu.VMEM((width, q_cols), BF16),
            pltpu.VMEM((width, head), BF16),
            pltpu.VMEM((width, head), BF16),
            pltpu.VMEM((q_cols, width), BF16),
            pltpu.VMEM((8, width), F32),
            pltpu.VMEM((blocks, 4 * q_cols // head, block), F32),
            pltpu.SemaphoreType.DMA((4,)),
            pltpu.SemaphoreType.DMA((blocks,)),
            pltpu.SemaphoreType.DMA((blocks,)),
            pltpu.SemaphoreType.DMA((blocks,)),
            pltpu.SemaphoreType.DMA((blocks,)),
        ],
        compiler_params=pltpu.CompilerParams(vmem_limit_bytes=(50 if layer else 58) * MIB),
    )(positions, freqs, hidden, gains, w_query, w_key, w_value, w_out, k_cache, v_cache)


def mlp_kernel(layer, n, row_chunks, col_chunks, o_ref, x_ref, gain_ref, wg_hbm, wu_hbm, wd_hbm, x_out,
               wg, wu, wd, part1, part2, acc_g, acc_u, g_sem, u_sem, d_sem, send1, recv1, send2, recv2):
    me = lax.axis_index("tp")
    batch, width = x_ref.shape
    ff = wg.shape[1]
    row_len = width // row_chunks
    col_len = width // col_chunks

    def g_in(i):
        rows = pl.ds(i * row_len, row_len)
        return pltpu.make_async_copy(wg_hbm.at[layer, rows, :], wg.at[rows, :], g_sem.at[i])

    def u_in(i):
        rows = pl.ds(i * row_len, row_len)
        return pltpu.make_async_copy(wu_hbm.at[layer, rows, :], wu.at[rows, :], u_sem.at[i])

    def d_in(i):
        cols = pl.ds(i * col_len, col_len)
        return pltpu.make_async_copy(wd_hbm.at[layer, :, cols], wd.at[:, cols], d_sem.at[i])

    for i in range(row_chunks):
        g_in(i).start()
        u_in(i).start()
    for i in range(col_chunks):
        d_in(i).start()

    barrier = pltpu.get_barrier_semaphore()
    peers = [lax.rem(me + k, n) for k in range(1, n)]
    for peer in peers:
        pl.semaphore_signal(barrier, inc=1, device_id={"tp": peer})
    pl.semaphore_wait(barrier, n - 1)

    def send(k, buf, cols, send_sem, recv_sem):
        return pltpu.make_async_remote_copy(
            src_ref=buf.at[me, :, cols], dst_ref=buf.at[me, :, cols], send_sem=send_sem, recv_sem=recv_sem,
            device_id={"tp": peers[k]})

    part1[me] = o_ref[...]
    all_cols = pl.ds(0, width)
    copies1 = [send(k, part1, all_cols, send1.at[k], recv1.at[k]) for k in range(n - 1)]
    for copy in copies1:
        copy.start()
    for copy in copies1:
        copy.wait_recv()

    def summed(buf):
        acc = buf[0].astype(F32)
        for j in range(1, n):
            acc = acc + buf[j].astype(F32)
        return acc[0:batch]

    gains = gain_ref[layer]
    normed = norm_rows(summed(part1), gains[1:2, :])
    mid = (x_ref[...].astype(F32) + normed.astype(F32)).astype(BF16)
    mid_f32 = mid.astype(F32)
    pre = norm_rows(mid_f32, gains[2:3, :])

    acc_g[...] = jnp.zeros_like(acc_g)
    acc_u[...] = jnp.zeros_like(acc_u)
    for i in range(row_chunks):
        rows = pl.ds(i * row_len, row_len)
        lhs = pre[:, i * row_len:(i + 1) * row_len]
        g_in(i).wait()
        acc_g[0:batch, :] += matmul(lhs, wg[rows, :])
        u_in(i).wait()
        acc_u[0:batch, :] += matmul(lhs, wu[rows, :])
    act = (jax.nn.gelu(acc_g[...], approximate=True) * acc_u[...]).astype(BF16)

    copies2 = []
    for i in range(col_chunks):
        cols = pl.ds(i * col_len, col_len)
        d_in(i).wait()
        down = matmul(act, wd[:, cols])
        part2[me, :, cols] = down[0:4].astype(BF16)
        for k in range(n - 1):
            copy = send(k, part2, cols, send2.at[i, k], recv2.at[i, k])
            copy.start()
            copies2.append(copy)
    for copy in copies2:
        copy.wait_recv()
    normed = norm_rows(summed(part2), gains[3:4, :])
    x_out[...] = (mid_f32 + normed.astype(F32)).astype(BF16)
    for copy in copies1 + copies2:
        copy.wait_send()


def mlp_call(layer, n, o_part, hidden, gains, w_gate, w_up, w_down):
    batch, width = hidden.shape
    ff = w_gate.shape[2]
    row_chunks, col_chunks = 8, 8
    vmem = pl.BlockSpec(memory_space=pltpu.VMEM)
    hbm = pl.BlockSpec(memory_space=pl.ANY)
    return pl.pallas_call(
        functools.partial(mlp_kernel, layer, n, row_chunks, col_chunks),
        name=f"mlp{layer}",
        out_shape=jax.ShapeDtypeStruct((batch, width), BF16),
        in_specs=[vmem, vmem, vmem, hbm, hbm, hbm],
        out_specs=vmem,
        scratch_shapes=[
            pltpu.VMEM((width, ff), BF16),
            pltpu.VMEM((width, ff), BF16),
            pltpu.VMEM((ff, width), BF16),
            pltpu.VMEM((n, 4, width), BF16),
            pltpu.VMEM((n, 4, width), BF16),
            pltpu.VMEM((8, ff), F32),
            pltpu.VMEM((8, ff), F32),
            pltpu.SemaphoreType.DMA((row_chunks,)),
            pltpu.SemaphoreType.DMA((row_chunks,)),
            pltpu.SemaphoreType.DMA((col_chunks,)),
            pltpu.SemaphoreType.DMA((n - 1,)),
            pltpu.SemaphoreType.DMA((n - 1,)),
            pltpu.SemaphoreType.DMA((col_chunks, n - 1)),
            pltpu.SemaphoreType.DMA((col_chunks, n - 1)),
        ],
        compiler_params=pltpu.CompilerParams(vmem_limit_bytes=50 * MIB, collective_id=layer, has_side_effects=True),
    )(o_part, hidden, gains, w_gate, w_up, w_down)


def decode_step(n, hidden, positions, k_local, v_local, k_global, v_global, w_query, w_key, w_value, w_out, w_gate, w_up, w_down, norm_scale):
    freqs = np.float32(ROPE_BASE) ** (np.float32(-2.0) * np.arange(HEAD // 2, dtype=np.float32) / np.float32(HEAD))
    freqs = jnp.asarray(np.concatenate([freqs, freqs])[None, :])
    flat = lambda cache: cache.reshape(cache.shape[0], cache.shape[1], HEAD)
    window = k_local.shape[1]
    o_part, k_loc, v_loc = attn_call(0, 1024, 4, window, positions, freqs, hidden, norm_scale, w_query, w_key, w_value, w_out, flat(k_local), flat(v_local))
    hidden = mlp_call(0, n, o_part, hidden, norm_scale, w_gate, w_up, w_down)
    o_part, k_glo, v_glo = attn_call(1, 2048, 6, 0, positions, freqs, hidden, norm_scale, w_query, w_key, w_value, w_out, flat(k_global), flat(v_global))
    hidden = mlp_call(1, n, o_part, hidden, norm_scale, w_gate, w_up, w_down)
    return (hidden, k_loc.reshape(k_local.shape), v_loc.reshape(v_local.shape), k_glo.reshape(k_global.shape), v_glo.reshape(v_global.shape))


def solution(mesh):
    row_spec = P('dp', None)
    cache_spec = P('dp', None, 'tp', None)
    col_split = P(None, None, 'tp')
    row_split = P(None, 'tp', None)
    in_specs = (row_spec, P('dp'), cache_spec, cache_spec, cache_spec, cache_spec, col_split, col_split, col_split, row_split, col_split, col_split, row_split, P())
    out_specs = (row_spec, cache_spec, cache_spec, cache_spec, cache_spec)
    body = functools.partial(decode_step, mesh.shape['tp'])
    return jax.shard_map(body, mesh=mesh, in_specs=in_specs, out_specs=out_specs, check_vma=False)
```

time: 236 us -> 88.7 us (0.38)
  blocking collectives: 95.9 us -> 0 us
  Pallas kernels: 0 us -> 86.5 us
  matrix products: 72.1 us -> 0 us
  other arithmetic: 49 us -> 0 us
  local copies, waits for them, and re-layouts: 16.7 us -> 1.39 us
    psum x4 -> x0, blocking collectives: 95.9 us -> none  [the longest x2 49.3 us: decoder_layer(): attn_sum = lax.psum(attn_part.astype(jnp.bfloat16), 'tp')]
    pallas_call x0 -> x4, Pallas kernels: none -> 86.5 us  [the longest x2 44.4 us: mlp_call(): pl.pallas_call(functools.partial(mlp_kernel, layer, n, row_chunks, col_ch...]
    dot_general x15 -> x0, matrix products: 69.7 us -> none  [the longest x2 23.4 us: mlp_part(): return jnp.dot(hidden_act, w_down, preferred_element_type=jnp.float32)]
    select_n x2 -> x0, other arithmetic: 40.2 us -> none  [project_and_store(): jnp.where(slot_hit, key_new.astype(jnp.bfloat16)[:, None], k_cache)]
    dot_general x3 -> x0, local copies, waits for them, and re-layouts: 16.6 us -> none  [project_and_store(): jnp.dot(normed, w_query, preferred_element_type=jnp.float32)]
    reduce_sum x9 -> x0, other arithmetic: 2.77 us -> none  [the longest x8 2.15 us: rms_norm(): jnp.mean(values_f32 * values_f32, axis=-1, keepdims=True) + NORM_EPS]
    sub x1 -> x0, matrix products: 2.4 us -> none  [attention(): attn_probs = jax.nn.softmax(logits, axis=-1).astype(jnp.bfloat16)]
where the time goes in v1:
time: 88.7 us; the launch traced here: 88.6 us
  Pallas kernels  86.5 us (98%)
  local copies, waits for them, and re-layouts  1.39 us (2%)
    pallas_call x2, Pallas kernels, mlp_call(): pl.pallas_call(functools.partial(mlp_kernel, layer, n, row_chunks, col_ch...  44.4 us
    pallas_call x2, Pallas kernels, attn_call(): pl.pallas_call(functools.partial(attn_kernel, layer, block, ahead, window...  42.1 us

profile of v1, /device:TPU:0, one launch (start us, length us, event | category | flops | bytes accessed | tf_op | source)
XLA Modules:
  0.0 88.6 jit_solution(15708694496424349467)
XLA Ops:
  0.6 0.0 copy-start.1
  0.6 0.0 copy-start.2
  0.7 11.3 %attn0.1 = (bf16[4,4096]{1,0:T(4,128)(2,1)}, bf16[3,4096,128]{2,1,0:T(8,128)(2,1)}, bf16[3,4096,128]{2,1,0:T(8,128)(2,1)}) custom-call(s32[3]{0:T(128)} %pos_ref.3, f32[1,128]{1,0:T(1,128)} %constant.2.clone.freq_ref, bf16[3,4096]{1,0:T(4,128)(2,1)} %x_ref.3, f32[2,4,4096]{2,1,0:T(4,128)} %gain_ref.7, bf16[2,4096,512]{2,1,0:T(8,128)(2,1)} %wq_hbm.3, ...), custom_call_target="tpu_custom_call" | custom-call | tf_op jit(solution)/shard_map/attn0/pallas_call | solution.py:177
  12.0 0.0 copy-done.1
  12.0 0.0 copy-done.2
  12.0 0.0 copy-start.3
  12.0 0.7 copy-done.3
  12.8 0.0 copy-start
  12.8 0.0 copy-start.4
  12.8 0.0 copy-start.5
  12.8 24.0 %mlp0.1.x_ref = bf16[3,4096]{1,0:T(4,128)(2,1)S(1)} custom-call(bf16[4,4096]{1,0:T(4,128)(2,1)S(1)} %copy-done.3, bf16[3,4096]{1,0:T(4,128)(2,1)S(1)} %copy-done.2, f32[2,4,4096]{2,1,0:T(4,128)S(1)} %copy-done.1, bf16[2,4096,1792]{2,1,0:T(8,128)(2,1)} %wg_hbm.3, bf16[2,4096,1792]{2,1,0:T(8,128)(2,1)} %wu_hbm.3, bf16[2,1792,4096]{2,1,0:T(8,128)(2,1)} %wd_hbm.3), custom_call_target="tpu_custom_call" | custom-call | tf_op jit(solution)/shard_map/mlp0/pallas_call | solution.py:294
  36.8 0.0 copy-done
  36.8 0.0 copy-done.4
  36.8 0.0 copy-done.5
  36.9 30.8 %attn1.1 = (bf16[4,4096]{1,0:T(4,128)(2,1)S(1)}, bf16[3,24576,128]{2,1,0:T(8,128)(2,1)}, bf16[3,24576,128]{2,1,0:T(8,128)(2,1)}) custom-call(s32[3]{0:T(128)S(1)} %copy-done.4, f32[1,128]{1,0:T(1,128)S(1)} %copy-done.5, bf16[3,4096]{1,0:T(4,128)(2,1)S(1)} %mlp0.1.x_ref, f32[2,4,4096]{2,1,0:T(4,128)S(1)} %copy-done.1, bf16[2,4096,512]{2,1,0:T(8,128)(2,1)} %wq_hbm.3, ...), custom_call_target="tpu_custom_call" | custom-call | tf_op jit(solution)/shard_map/attn1/pallas_call | solution.py:177
  67.7 20.3 %mlp1.1 = bf16[3,4096]{1,0:T(4,128)(2,1)S(1)} custom-call(bf16[4,4096]{1,0:T(4,128)(2,1)S(1)} %get-tuple-element.12.o_ref, bf16[3,4096]{1,0:T(4,128)(2,1)S(1)} %mlp0.1.x_ref, f32[2,4,4096]{2,1,0:T(4,128)S(1)} %copy-done.1, bf16[2,4096,1792]{2,1,0:T(8,128)(2,1)} %wg_hbm.3, bf16[2,4096,1792]{2,1,0:T(8,128)(2,1)} %wu_hbm.3, bf16[2,1792,4096]{2,1,0:T(8,128)(2,1)} %wd_hbm.3), custom_call_target="tpu_custom_call" | custom-call | tf_op jit(solution)/shard_map/mlp1/pallas_call | solution.py:294
  88.0 0.6 copy.25
Async XLA Ops:
  0.6 11.4 %copy-start.1 = (f32[2,4,4096]{2,1,0:T(4,128)S(1)}, f32[2,4,4096]{2,1,0:T(4,128)}, u32[]{:S(2)}) copy-start(f32[2,4,4096]{2,1,0:T(4,128)} %gain_ref.7) | copy-start | bytes 393220
  0.6 11.4 %copy-start.2 = (bf16[3,4096]{1,0:T(4,128)(2,1)S(1)}, bf16[3,4096]{1,0:T(4,128)(2,1)}, u32[]{:S(2)}) copy-start(bf16[3,4096]{1,0:T(4,128)(2,1)} %x_ref.3) | copy-start | bytes 73732
  12.0 0.8 copy-start.3
  12.8 24.1 %copy-start = (bf16[2,4096,128]{2,1,0:T(8,128)(2,1)S(1)}, bf16[2,4096,128]{2,1,0:T(8,128)(2,1)}, u32[]{:S(2)}) copy-start(bf16[2,4096,128]{2,1,0:T(8,128)(2,1)} %wk_hbm.3) | copy-start | bytes 6291460
  12.8 24.1 %copy-start.4 = (s32[3]{0:T(128)S(1)}, s32[3]{0:T(128)}, u32[]{:S(2)}) copy-start(s32[3]{0:T(128)} %pos_ref.3) | copy-start | bytes 40
  12.8 24.1 %copy-start.5 = (f32[1,128]{1,0:T(1,128)S(1)}, f32[1,128]{1,0:T(1,128)}, u32[]{:S(2)}) copy-start(f32[1,128]{1,0:T(1,128)} %constant.2.clone.freq_ref) | copy-start | bytes 1540

commit v2 on v1

v2 whole, which is shorter than its diff:
```python
import functools

import jax
import jax.numpy as jnp
import numpy as np
from jax import lax
from jax.experimental import pallas as pl
from jax.experimental.pallas import tpu as pltpu
from jax.sharding import PartitionSpec as P

SOFT_CAP = 50.0
NORM_EPS = 1e-6
ROPE_BASE = 10000.0
HEAD = 128
MIB = 1024 * 1024
AHEAD, EARLY1, EARLY2 = 99, 0, 0
F32 = jnp.float32
BF16 = jnp.bfloat16


def in_vmem(value):
    return pltpu.with_memory_space_constraint(value, pltpu.VMEM)


def in_hbm(value):
    return pltpu.with_memory_space_constraint(value, pltpu.HBM)


def norm_rows(values, gain_row):
    inv_rms = lax.rsqrt(jnp.mean(values * values, axis=-1, keepdims=True) + NORM_EPS)
    return (values * inv_rms * (1.0 + gain_row)).astype(BF16)


def matmul(lhs, rhs):
    return jnp.dot(lhs, rhs, preferred_element_type=F32)


def rotate(head, cos_part, sin_part):
    return head * cos_part + pltpu.roll(head, HEAD // 2, 1) * sin_part


def attn_kernel(layer, block, window, k_kept, pos_hbm, freq_hbm, x_in, gain_hbm, wq_hbm, wk_hbm, wv_hbm, wo_hbm, k_in, v_hbm,
                o_ref, k_out, v_out, *scratch):
    if k_kept:
        kbuf = k_in
        scratch = scratch[:7] + (x_in,) + scratch[7:]
    else:
        kbuf, scratch = scratch[0], scratch[1:]
    vbuf, wq, wk, wv, wo, pos_ref, freq_ref, x_ref, gain_ref, xbuf, ebuf, tiles, load_sem, t_sem, kout_sem, vout_sem = scratch
    batch, length = v_hbm.shape[0], v_hbm.shape[1]
    heads = wq.shape[1] // HEAD
    blocks = length // block

    def piece(i):
        return pl.ds(pl.multiple_of(i * block, block), block)

    def k_load(i):
        return pltpu.make_async_copy(k_in.at[:, piece(i), :], kbuf.at[:, piece(i), :], load_sem.at[8 + i])

    def v_load(i):
        return pltpu.make_async_copy(v_hbm.at[:, piece(i), :], vbuf.at[:, piece(i), :], load_sem.at[8 + blocks + i])

    def k_back(i):
        return pltpu.make_async_copy(kbuf.at[:, piece(i), :], k_out.at[:, piece(i), :], kout_sem.at[i])

    def v_back(i):
        return pltpu.make_async_copy(vbuf.at[:, piece(i), :], v_out.at[:, piece(i), :], vout_sem.at[i])

    pos_copy = pltpu.make_async_copy(pos_hbm, pos_ref, load_sem.at[0])
    freq_copy = pltpu.make_async_copy(freq_hbm, freq_ref, load_sem.at[1])
    if not k_kept:
        x_copy = pltpu.make_async_copy(x_in, x_ref, load_sem.at[2])
    gain_copy = pltpu.make_async_copy(gain_hbm.at[layer], gain_ref, load_sem.at[3])
    wq_copy = pltpu.make_async_copy(wq_hbm.at[layer], wq, load_sem.at[4])
    wk_copy = pltpu.make_async_copy(wk_hbm.at[layer], wk, load_sem.at[5])
    wv_copy = pltpu.make_async_copy(wv_hbm.at[layer], wv, load_sem.at[6])
    wo_copy = pltpu.make_async_copy(wo_hbm.at[layer], wo, load_sem.at[7])
    first = (gain_copy, pos_copy, freq_copy, wk_copy, wq_copy, wv_copy)
    for copy in first if k_kept else (x_copy,) + first:
        copy.start()
    if not k_kept:
        for i in range(blocks):
            k_load(i).start()
    for i in range(blocks):
        v_load(i).start()
    wo_copy.start()

    xbuf[...] = jnp.zeros_like(xbuf)
    if not k_kept:
        x_copy.wait()
    gain_copy.wait()
    xbuf[0:batch, :] = x_ref[...].astype(F32)
    normed = norm_rows(xbuf[...], gain_ref[0:1, :])

    pos_copy.wait()
    freq_copy.wait()
    row_id = lax.broadcasted_iota(jnp.int32, (8, HEAD), 0)
    pos_rows = jnp.full((8, HEAD), pos_ref[0], jnp.int32)
    for b in range(1, batch):
        pos_rows = jnp.where(row_id == b, pos_ref[b], pos_rows)
    angles = pos_rows.astype(F32) * freq_ref[...]
    lane_id = lax.broadcasted_iota(jnp.int32, (8, HEAD), 1)
    cos_part = jnp.cos(angles)
    sin_part = jnp.sin(angles)
    sin_part = jnp.where(lane_id < HEAD // 2, -sin_part, sin_part)

    wk_copy.wait()
    key_new = rotate(matmul(normed, wk[...]), cos_part, sin_part).astype(BF16)
    wq_copy.wait()
    queries = matmul(normed, wq[...])
    stacked = jnp.concatenate([rotate(queries[:, h * HEAD:(h + 1) * HEAD], cos_part, sin_part)[0:4] for h in range(heads)], axis=0)
    rows = 4 * heads
    of_row = lax.broadcasted_iota(jnp.int32, (rows, HEAD), 0) % 4
    lhs = jnp.concatenate([jnp.where(of_row == b, stacked, 0.0) for b in range(batch)], axis=1).astype(BF16)
    wv_copy.wait()
    if k_kept:
        for i in range(blocks):
            k_back(i).start()
    value_new = matmul(normed, wv[...]).astype(BF16)

    slots = [pos_ref[b] % window if window else pos_ref[b] for b in range(batch)]
    tile_rows = lax.broadcasted_iota(jnp.int32, (16, HEAD), 0)

    def put_row(buf, new_rows, i):
        for b in range(batch):
            @pl.when(slots[b] // block == i)
            def _():
                base = pl.multiple_of((slots[b] // 16) * 16, 16)
                tile = buf[b, pl.ds(base, 16), :]
                new_row = jnp.broadcast_to(new_rows[b:b + 1, :].astype(F32), (16, HEAD))
                kept = tile.astype(F32)
                buf[b, pl.ds(base, 16), :] = jnp.where(tile_rows == slots[b] - base, new_row, kept).astype(BF16)

    if k_kept:
        key_rows = jnp.concatenate([key_new[0:4]] * heads, axis=0).astype(F32)
        new_logits = jnp.sum(stacked.astype(BF16).astype(F32) * key_rows, axis=-1, keepdims=True) * HEAD ** -0.5
        new_weights = jnp.exp(SOFT_CAP * jnp.tanh(new_logits / SOFT_CAP))

    col_ids = lax.broadcasted_iota(jnp.int32, (rows, block), 1)
    of_col = lax.broadcasted_iota(jnp.int32, (rows, block), 0) % 4
    limits = jnp.full((rows, block), pos_ref[0], jnp.int32)
    for b in range(1, batch):
        limits = jnp.where(of_col == b, pos_ref[b], limits)

    def score_step(i, total):
        if not k_kept:
            k_load(i).wait()
            put_row(kbuf, key_new, i)
        keys = jnp.concatenate([kbuf[b, piece(i), :] for b in range(batch)], axis=1)
        logits = lax.dot_general(lhs, keys, (((1,), (1,)), ((), ())), preferred_element_type=F32) * HEAD ** -0.5
        weights = jnp.exp(SOFT_CAP * jnp.tanh(logits / SOFT_CAP))
        if k_kept:
            col_pos = col_ids + i * block
            weights = jnp.where(col_pos < limits, weights, jnp.where(col_pos == limits, new_weights, 0.0))
        ebuf[i] = weights
        if not k_kept:
            k_back(i).start()
        return total + jnp.sum(weights, axis=-1, keepdims=True)

    total = lax.fori_loop(0, blocks, score_step, jnp.zeros((rows, 1), F32))
    inv_total = 1.0 / total

    def value_step(i, acc):
        v_load(i).wait()
        put_row(vbuf, value_new, i)
        values = jnp.concatenate([vbuf[b, piece(i), :] for b in range(batch)], axis=1)
        probs = (ebuf[i] * inv_total).astype(BF16)
        out = acc + matmul(probs, values)
        v_back(i).start()
        return out

    mixed = lax.fori_loop(0, blocks, value_step, jnp.zeros((rows, batch * HEAD), F32))
    tile_copies = []
    if k_kept:
        for i in range(blocks):
            k_back(i).wait()
        for b in range(batch):
            base = pl.multiple_of((slots[b] // 16) * 16, 16)
            tile = kbuf[b, pl.ds(base, 16), :].astype(F32)
            new_row = jnp.broadcast_to(key_new[b:b + 1, :].astype(F32), (16, HEAD))
            tiles[b] = jnp.where(tile_rows == slots[b] - base, new_row, tile).astype(BF16)
            tile_copies.append(pltpu.make_async_copy(tiles.at[b], k_out.at[b, pl.ds(base, 16), :], t_sem.at[b]))
    picked = jnp.zeros((rows, HEAD), F32)
    for b in range(batch):
        picked = jnp.where(of_row == b, mixed[:, b * HEAD:(b + 1) * HEAD], picked)
    merged = jnp.concatenate([picked[4 * h:4 * h + 4, :] for h in range(heads)], axis=1).astype(BF16)
    for copy in tile_copies:
        copy.start()
    wo_copy.wait()
    o_ref[...] = matmul(merged, wo[...]).astype(BF16)

    def drain(i, carry):
        if not k_kept:
            k_back(i).wait()
        v_back(i).wait()
        return carry

    lax.fori_loop(0, blocks, drain, 0)
    for copy in tile_copies:
        copy.wait()


def attn_call(layer, block, window, k_kept, positions, freqs, hidden, gains, w_query, w_key, w_value, w_out, k_cache, v_cache):
    batch, length, head = v_cache.shape
    width, q_cols = w_query.shape[1:]
    blocks = length // block
    vmem = pl.BlockSpec(memory_space=pltpu.VMEM)
    hbm = pl.BlockSpec(memory_space=pl.ANY)
    cache = jax.ShapeDtypeStruct(v_cache.shape, v_cache.dtype)
    kbuf = [] if k_kept else [pltpu.VMEM(v_cache.shape, BF16)]
    return pl.pallas_call(
        functools.partial(attn_kernel, layer, block, window, k_kept),
        name=f"attn{layer}",
        out_shape=(pltpu.VMEM((4, width), BF16), cache, cache),
        in_specs=[hbm, hbm, vmem if k_kept else hbm] + [hbm] * 5 + [vmem if k_kept else hbm, hbm],
        out_specs=(vmem, hbm, hbm),
        scratch_shapes=kbuf + [
            pltpu.VMEM(v_cache.shape, BF16),
            pltpu.VMEM((width, q_cols), BF16),
            pltpu.VMEM((width, head), BF16),
            pltpu.VMEM((width, head), BF16),
            pltpu.VMEM((q_cols, width), BF16),
            pltpu.SMEM((batch,), jnp.int32),
            pltpu.VMEM((1, head), F32),
        ] + ([] if k_kept else [pltpu.VMEM((batch, width), BF16)]) + [
            pltpu.VMEM((4, width), F32),
            pltpu.VMEM((8, width), F32),
            pltpu.VMEM((blocks, 4 * q_cols // head, block), F32),
            pltpu.VMEM((batch, 16, head), BF16),
            pltpu.SemaphoreType.DMA((8 + 2 * blocks,)),
            pltpu.SemaphoreType.DMA((batch,)),
            pltpu.SemaphoreType.DMA((blocks,)),
            pltpu.SemaphoreType.DMA((blocks,)),
        ],
        compiler_params=pltpu.CompilerParams(vmem_limit_bytes=int((45 if layer else 60) * MIB)),
    )(*(in_hbm(value) for value in (positions, freqs)), (in_vmem if k_kept else in_hbm)(hidden),
      *(in_hbm(value) for value in (gains, w_query, w_key, w_value, w_out)), (in_vmem if k_kept else in_hbm)(k_cache), in_hbm(v_cache))


def mlp_kernel(layer, n, row_chunks, col_chunks, k_pieces, o_ref, x_in, gain_hbm, wg_hbm, wu_hbm, wd_hbm, *refs):
    if k_pieces:
        k_hbm, x_out, k_pre = refs[:3]
        refs = refs[3:]
    else:
        x_out, refs = refs[0], refs[1:]
    if layer:
        x_ref = x_in
    else:
        x_ref, refs = refs[0], refs[1:]
    wg, wu, wd, gain_ref, part1, part2, acc_g, acc_u, load_sem, send1, recv1, send2, recv2 = refs
    me = lax.axis_index("tp")
    batch, width = x_ref.shape
    row_len = width // row_chunks
    col_len = width // col_chunks
    row_dots, col_dots, ahead, early1, early2 = 2, 4, AHEAD, EARLY1, EARLY2

    def g_in(i):
        rows = pl.ds(i * row_len, row_len)
        return pltpu.make_async_copy(wg_hbm.at[layer, rows, :], wg.at[rows, :], load_sem.at[2 + i])

    def u_in(i):
        rows = pl.ds(i * row_len, row_len)
        return pltpu.make_async_copy(wu_hbm.at[layer, rows, :], wu.at[rows, :], load_sem.at[2 + row_chunks + i])

    def d_in(i):
        cols = pl.ds(i * col_len, col_len)
        return pltpu.make_async_copy(wd_hbm.at[layer, :, cols], wd.at[:, cols], load_sem.at[2 + 2 * row_chunks + i])

    if not layer:
        x_copy = pltpu.make_async_copy(x_in, x_ref, load_sem.at[0])
    gain_copy = pltpu.make_async_copy(gain_hbm.at[layer], gain_ref, load_sem.at[1])
    k_copies = []
    for i in range(k_pieces):
        k_len = k_hbm.shape[1] // k_pieces
        slots = pl.ds(i * k_len, k_len)
        k_copies.append(pltpu.make_async_copy(k_hbm.at[:, slots, :], k_pre.at[:, slots, :], load_sem.at[2 + 2 * row_chunks + col_chunks + i]))
    loads = []
    for d in range(row_dots):
        span = range(d * row_chunks // row_dots, (d + 1) * row_chunks // row_dots)
        loads += [g_in(i) for i in span] + [u_in(i) for i in span]
    loads += [d_in(i) for i in range(col_chunks)] + k_copies
    arrived = 0

    def wait_loads(count):
        nonlocal arrived
        while arrived < min(count, len(loads)):
            loads[arrived].wait()
            if arrived + ahead < len(loads):
                loads[arrived + ahead].start()
            arrived += 1

    if not layer:
        x_copy.start()
    gain_copy.start()
    for load in loads[:ahead]:
        load.start()

    barrier = pltpu.get_barrier_semaphore()
    peers = [lax.rem(me // 4 + far // 4, 2) * 4 + lax.rem(me // 2 + far // 2, 2) * 2 + lax.rem(me + far, 2) for far in (6, 7, 4, 5, 2, 3, 1)]
    for peer in peers:
        pl.semaphore_signal(barrier, inc=1, device_id={"tp": peer})
    pl.semaphore_wait(barrier, n - 1)

    def send(k, buf, cols, send_sem, recv_sem):
        return pltpu.make_async_remote_copy(
            src_ref=buf.at[me, :, cols], dst_ref=buf.at[me, :, cols], send_sem=send_sem, recv_sem=recv_sem,
            device_id={"tp": peers[k]})

    part1[me] = o_ref[...]
    all_cols = pl.ds(0, width)
    copies1 = [send(k, part1, all_cols, send1.at[k], recv1.at[k]) for k in range(n - 1)]
    for copy in copies1:
        copy.start()
    if not layer:
        x_copy.wait()
    gain_copy.wait()
    wait_loads(early1)
    for copy in copies1:
        copy.wait_recv()

    def summed(buf):
        acc = buf[0].astype(F32)
        for j in range(1, n):
            acc = acc + buf[j].astype(F32)
        return acc[0:batch]

    normed = norm_rows(summed(part1), gain_ref[1:2, :])
    mid = (x_ref[...].astype(F32) + normed.astype(F32)).astype(BF16)
    mid_f32 = mid.astype(F32)
    pre = norm_rows(mid_f32, gain_ref[2:3, :])

    for d in range(row_dots):
        first, last = d * row_chunks // row_dots, (d + 1) * row_chunks // row_dots
        rows = slice(first * row_len, last * row_len)
        lhs = pre[:, rows]
        wait_loads(first + last)
        gate = matmul(lhs, wg[rows, :])
        acc_g[0:batch, :] = gate if d == 0 else acc_g[0:batch, :] + gate
        wait_loads(2 * last)
        up = matmul(lhs, wu[rows, :])
        acc_u[0:batch, :] = up if d == 0 else acc_u[0:batch, :] + up
    act = (jax.nn.gelu(acc_g[0:batch, :], approximate=True) * acc_u[0:batch, :]).astype(BF16)

    copies2 = []
    for d in range(col_dots):
        first, last = d * col_chunks // col_dots, (d + 1) * col_chunks // col_dots
        wait_loads(2 * row_chunks + last)
        down = matmul(act, wd[:, first * col_len:last * col_len])
        cols = pl.ds(first * col_len, (last - first) * col_len)
        part2[me, 0:batch, cols] = down.astype(BF16)
        for k in range(n - 1):
            copy = send(k, part2, cols, send2.at[d, k], recv2.at[d, k])
            copy.start()
            copies2.append(copy)
    wait_loads(2 * row_chunks + col_chunks + early2)
    for copy in copies2:
        copy.wait_recv()
    normed = norm_rows(summed(part2), gain_ref[3:4, :])
    x_out[...] = (mid_f32 + normed.astype(F32)).astype(BF16)
    for copy in copies1 + copies2:
        copy.wait_send()
    wait_loads(len(loads))


def mlp_call(layer, n, k_pieces, o_part, hidden, gains, w_gate, w_up, w_down, *k_cache):
    batch, width = hidden.shape
    ff = w_gate.shape[2]
    row_chunks, col_chunks = 8, 8
    vmem = pl.BlockSpec(memory_space=pltpu.VMEM)
    hbm = pl.BlockSpec(memory_space=pl.ANY)
    kept = tuple(pltpu.VMEM(cache.shape, cache.dtype) for cache in k_cache)
    return pl.pallas_call(
        functools.partial(mlp_kernel, layer, n, row_chunks, col_chunks, k_pieces),
        name=f"mlp{layer}",
        out_shape=((jax.ShapeDtypeStruct if layer else pltpu.VMEM)((batch, width), BF16),) + kept,
        in_specs=[vmem, vmem if layer else hbm] + [hbm] * (4 + len(kept)),
        out_specs=(vmem,) * (1 + len(kept)),
        scratch_shapes=([] if layer else [pltpu.VMEM((batch, width), BF16)]) + [
            pltpu.VMEM((width, ff), BF16),
            pltpu.VMEM((width, ff), BF16),
            pltpu.VMEM((ff, width), BF16),
            pltpu.VMEM((4, width), F32),
            pltpu.VMEM((n, 4, width), BF16),
            pltpu.VMEM((n, 4, width), BF16),
            pltpu.VMEM((8, ff), F32),
            pltpu.VMEM((8, ff), F32),
            pltpu.SemaphoreType.DMA((2 + 2 * row_chunks + col_chunks + k_pieces,)),
            pltpu.SemaphoreType.DMA((n - 1,)),
            pltpu.SemaphoreType.DMA((n - 1,)),
            pltpu.SemaphoreType.DMA((col_chunks, n - 1)),
            pltpu.SemaphoreType.DMA((col_chunks, n - 1)),
        ],
        compiler_params=pltpu.CompilerParams(vmem_limit_bytes=int(44 * MIB), collective_id=layer, has_side_effects=True),
    )(in_vmem(o_part), (in_vmem if layer else in_hbm)(hidden), *(in_hbm(value) for value in (gains, w_gate, w_up, w_down) + k_cache))


def decode_step(n, hidden, positions, k_local, v_local, k_global, v_global, w_query, w_key, w_value, w_out, w_gate, w_up, w_down, norm_scale):
    freqs = np.float32(ROPE_BASE) ** (np.float32(-2.0) * np.arange(HEAD // 2, dtype=np.float32) / np.float32(HEAD))
    freqs = jnp.asarray(np.concatenate([freqs, freqs])[None, :])
    flat = lambda cache: cache.reshape(cache.shape[0], cache.shape[1], HEAD)
    window = k_local.shape[1]
    shared = (positions, freqs)
    weights = (norm_scale, w_query, w_key, w_value, w_out)
    o_part, k_loc, v_loc = attn_call(0, 2048, window, False, *shared, hidden, *weights, flat(k_local), flat(v_local))
    hidden, k_pre = mlp_call(0, n, 12, o_part, hidden, norm_scale, w_gate, w_up, w_down, flat(k_global))
    o_part, k_glo, v_glo = attn_call(1, 4096, 0, True, *shared, hidden, *weights, k_pre, flat(v_global))
    hidden, = mlp_call(1, n, 0, o_part, hidden, norm_scale, w_gate, w_up, w_down)
    return (hidden, k_loc.reshape(k_local.shape), v_loc.reshape(v_local.shape), k_glo.reshape(k_global.shape), v_glo.reshape(v_global.shape))


def solution(mesh):
    row_spec = P('dp', None)
    cache_spec = P('dp', None, 'tp', None)
    col_split = P(None, None, 'tp')
    row_split = P(None, 'tp', None)
    in_specs = (row_spec, P('dp'), cache_spec, cache_spec, cache_spec, cache_spec, col_split, col_split, col_split, row_split, col_split, col_split, row_split, P())
    out_specs = (row_spec, cache_spec, cache_spec, cache_spec, cache_spec)
    body = functools.partial(decode_step, mesh.shape['tp'])
    return jax.shard_map(body, mesh=mesh, in_specs=in_specs, out_specs=out_specs, check_vma=False)
```

time: 88.7 us -> 75.6 us (0.85)
  Pallas kernels: 86.5 us -> 74.2 us
    pallas_call x2, Pallas kernels: 42.1 us -> 31.8 us  [attn_call(): pl.pallas_call(functools.partial(attn_kernel, layer, block, window, k_kep...]
    pallas_call x2, Pallas kernels: 44.4 us -> 42.4 us  [mlp_call(): pl.pallas_call(functools.partial(mlp_kernel, layer, n, row_chunks, col_ch...]
where the time goes in v2:
time: 75.6 us; the launch traced here: 75.5 us
  Pallas kernels  74.2 us (98%)
    pallas_call x2, Pallas kernels, mlp_call(): pl.pallas_call(functools.partial(mlp_kernel, layer, n, row_chunks, col_ch...  42.4 us
    pallas_call x2, Pallas kernels, attn_call(): pl.pallas_call(functools.partial(attn_kernel, layer, block, window, k_kep...  31.8 us

profile of v2, /device:TPU:0, one launch (start us, length us, event | category | flops | bytes accessed | tf_op | source)
XLA Modules:
  0.0 75.5 jit_solution(13621710807337494828)
XLA Ops:
  0.6 9.0 %attn0.1 = (bf16[4,4096]{1,0:T(4,128)(2,1)S(1)}, bf16[3,4096,128]{2,1,0:T(8,128)(2,1)}, bf16[3,4096,128]{2,1,0:T(8,128)(2,1)}) custom-call(s32[3]{0:T(128)} %pos_hbm.3, f32[1,128]{1,0:T(1,128)} %constant.2.clone.freq_hbm, bf16[3,4096]{1,0:T(4,128)(2,1)} %x_in.3, f32[2,4,4096]{2,1,0:T(4,128)} %gain_hbm.7, bf16[2,4096,512]{2,1,0:T(8,128)(2,1)} %wq_hbm.3, ...), custom_call_target="tpu_custom_call" | custom-call | tf_op jit(solution)/shard_map/attn0/pallas_call | solution.py:211
  9.6 22.0 %mlp0.1 = (bf16[3,4096]{1,0:T(4,128)(2,1)S(1)}, bf16[3,24576,128]{2,1,0:T(8,128)(2,1)S(1)}) custom-call(bf16[4,4096]{1,0:T(4,128)(2,1)S(1)} %get-tuple-element.13.o_ref, bf16[3,4096]{1,0:T(4,128)(2,1)} %x_in.3, f32[2,4,4096]{2,1,0:T(4,128)} %gain_hbm.7, bf16[2,4096,1792]{2,1,0:T(8,128)(2,1)} %wg_hbm.3, bf16[2,4096,1792]{2,1,0:T(8,128)(2,1)} %wu_hbm.3, ...), custom_call_target="tpu_custom_call" | custom-call | tf_op jit(solution)/shard_map/mlp0/pallas_call | solution.py:372
  31.6 22.8 %attn1.1 = (bf16[4,4096]{1,0:T(4,128)(2,1)S(1)}, bf16[3,24576,128]{2,1,0:T(8,128)(2,1)}, bf16[3,24576,128]{2,1,0:T(8,128)(2,1)}) custom-call(s32[3]{0:T(128)} %pos_hbm.3, f32[1,128]{1,0:T(1,128)} %constant.2.clone.freq_hbm, bf16[3,4096]{1,0:T(4,128)(2,1)S(1)} %get-tuple-element.14.x_in, f32[2,4,4096]{2,1,0:T(4,128)} %gain_hbm.7, ...), custom_call_target="tpu_custom_call" | custom-call | tf_op jit(solution)/shard_map/attn1/pallas_call | solution.py:211
  54.4 20.4 %mlp1.1 = bf16[3,4096]{1,0:T(4,128)(2,1)S(1)} custom-call(bf16[4,4096]{1,0:T(4,128)(2,1)S(1)} %get-tuple-element.16.o_ref, bf16[3,4096]{1,0:T(4,128)(2,1)S(1)} %get-tuple-element.14.x_in, f32[2,4,4096]{2,1,0:T(4,128)} %gain_hbm.7, bf16[2,4096,1792]{2,1,0:T(8,128)(2,1)} %wg_hbm.3, bf16[2,4096,1792]{2,1,0:T(8,128)(2,1)} %wu_hbm.3, bf16[2,1792,4096]{2,1,0:T(8,128)(2,1)} %wd_hbm.3), custom_call_target="tpu_custom_call" | custom-call | tf_op jit(solution)/shard_map/mlp1/pallas_call | solution.py:372
  74.9 0.6 copy.25

commit v3 on v0

v3 whole, which is shorter than its diff:
```python
import functools

import jax
import jax.numpy as jnp
import numpy as np
from jax import lax
from jax.experimental import pallas as pl
from jax.experimental.pallas import tpu as pltpu
from jax.sharding import PartitionSpec as P

SOFT_CAP = 50.0
NORM_EPS = 1e-6
ROPE_BASE = 10000.0
HEAD = 128
MIB = 1024 * 1024
F32 = jnp.float32
BF16 = jnp.bfloat16
ROW_CHUNKS, ROW_DOTS = 8, 2
COL_CHUNKS, COL_DOTS = 8, 4
K_EARLY = 4
K_PIECES = 12
LOCAL_BLOCKS = 2
LAYER0_MIB, ATTN_MIB = 32, 32
QKV_CHUNKS = 4
COPY = pltpu.make_async_copy


def in_vmem(value):
    return pltpu.with_memory_space_constraint(value, pltpu.VMEM)


def in_hbm(value):
    return pltpu.with_memory_space_constraint(value, pltpu.HBM)


def norm_rows(values, gain_row):
    inv_rms = lax.rsqrt(jnp.mean(values * values, axis=-1, keepdims=True) + NORM_EPS)
    return (values * inv_rms * (1.0 + gain_row)).astype(BF16)


def matmul(lhs, rhs):
    return jnp.dot(lhs, rhs, preferred_element_type=F32)


def capped_exp(logits):
    return jnp.exp(SOFT_CAP * jnp.tanh(logits * HEAD ** -0.5 / SOFT_CAP))


def rotate(head, cos_part, sin_part):
    return head * cos_part + pltpu.roll(head, HEAD // 2, 1) * sin_part


def rope_tables(pos_ref, freq_ref, batch):
    row_id = lax.broadcasted_iota(jnp.int32, (8, HEAD), 0)
    pos_rows = jnp.full((8, HEAD), pos_ref[0], jnp.int32)
    for b in range(1, batch):
        pos_rows = jnp.where(row_id == b, pos_ref[b], pos_rows)
    angles = pos_rows.astype(F32) * freq_ref[...]
    lane_id = lax.broadcasted_iota(jnp.int32, (8, HEAD), 1)
    sin_part = jnp.sin(angles)
    return jnp.cos(angles), jnp.where(lane_id < HEAD // 2, -sin_part, sin_part)


def row_of(rows):
    return lax.broadcasted_iota(jnp.int32, (rows, HEAD), 0) % 4


def stack_queries(queries, tables, heads, batch):
    stacked = jnp.concatenate([rotate(queries[:, h * HEAD:(h + 1) * HEAD], *tables)[0:4] for h in range(heads)], axis=0)
    of_row = row_of(4 * heads)
    lhs = jnp.concatenate([jnp.where(of_row == b, stacked, 0.0) for b in range(batch)], axis=1).astype(BF16)
    return stacked.astype(BF16).astype(F32), lhs


def per_head(new_rows, heads):
    return jnp.concatenate([new_rows[0:4]] * heads, axis=0).astype(F32)


def row_values(values, rows, cols):
    of_col = lax.broadcasted_iota(jnp.int32, (rows, cols), 0) % 4
    out = jnp.full((rows, cols), values[0], jnp.int32)
    for b in range(1, len(values)):
        out = jnp.where(of_col == b, values[b], out)
    return out


def pick_rows(mixed, heads, batch):
    of_row = row_of(4 * heads)
    picked = jnp.zeros((4 * heads, HEAD), F32)
    for b in range(batch):
        picked = jnp.where(of_row == b, mixed[:, b * HEAD:(b + 1) * HEAD], picked)
    return picked


def merge_heads(picked, heads):
    return jnp.concatenate([picked[4 * h:4 * h + 4, :] for h in range(heads)], axis=1).astype(BF16)


def score_rows(lhs, keys):
    return lax.dot_general(lhs, keys, (((1,), (1,)), ((), ())), preferred_element_type=F32)


class Loads:
    def __init__(self, sem):
        self.sem, self.count = sem, 0

    def add(self, src, dst):
        self.count += 1
        return COPY(src, dst, self.sem.at[self.count - 1])


def start_all(copies):
    for copy in copies:
        copy.start()


def wait_all(copies):
    for copy in copies:
        copy.wait()


class Exchange:
    def __init__(self, n, me, buf, send_sem, recv_sem):
        self.me, self.n, self.buf, self.send_sem, self.recv_sem = me, n, buf, send_sem, recv_sem
        self.peers = [lax.rem(me // 4 + far // 4, 2) * 4 + lax.rem(me // 2 + far // 2, 2) * 2 + lax.rem(me + far, 2) for far in (6, 7, 4, 5, 2, 3, 1)]
        self.sent = []

    def send(self, first, last):
        cols, i, group = pl.ds(first, last - first), len(self.sent), []
        for k, peer in enumerate(self.peers):
            group.append(pltpu.make_async_remote_copy(
                src_ref=self.buf.at[self.me, :, cols], dst_ref=self.buf.at[self.me, :, cols],
                send_sem=self.send_sem.at[i, k], recv_sem=self.recv_sem.at[i, k], device_id={"tp": peer}))
            group[k].start()
        self.sent.append((group, first, last))

    def summed(self, batch):
        parts = []
        for group, first, last in self.sent:
            for copy in group:
                copy.wait_recv()
            acc = self.buf[0, :, first:last].astype(F32)
            for j in range(1, self.n):
                acc = acc + self.buf[j, :, first:last].astype(F32)
            parts.append(acc)
        return jnp.concatenate(parts, axis=1)[0:batch]

    def drain(self):
        for group, _, _ in self.sent:
            for copy in group:
                copy.wait_send()


def row_loads(loads, hbm, layer, buf):
    step = buf.shape[0] // ROW_CHUNKS
    return [loads.add(hbm.at[layer, pl.ds(i * step, step), :], buf.at[pl.ds(i * step, step), :]) for i in range(ROW_CHUNKS)]


def mlp_tail(branch, hidden, gain_ref, gate, up, order, after, down_dots, wg, wu, acc_g, acc_u, exchange):
    batch, width = hidden.shape
    mid = (hidden + norm_rows(branch, gain_ref[1:2, :]).astype(F32)).astype(BF16).astype(F32)
    pre = norm_rows(mid, gain_ref[2:3, :])
    part = ROW_CHUNKS // ROW_DOTS
    row_len = width // ROW_DOTS
    for kind, d in order:
        loads, weights, acc = (gate, wg, acc_g) if kind == 0 else (up, wu, acc_u)
        wait_all(loads[d * part:(d + 1) * part])
        rows = slice(d * row_len, (d + 1) * row_len)
        product = matmul(pre[:, rows], weights[rows, :])
        acc[0:batch, :] = product if d == 0 else acc[0:batch, :] + product
        start_all(after.get((kind, d), []))
    act = (jax.nn.gelu(acc_g[0:batch, :], approximate=True) * acc_u[0:batch, :]).astype(BF16)
    first = 0
    for loads, buf, row, col, cols in down_dots:
        wait_all(loads)
        last = first + cols
        exchange.buf[exchange.me, 0:batch, first:last] = matmul(act, buf[row:row + act.shape[1], col:col + cols]).astype(BF16)
        exchange.send(first, last)
        first = last
    total = exchange.summed(batch)
    return (mid + norm_rows(total, gain_ref[3:4, :]).astype(F32)).astype(BF16)


def greet(exchange):
    barrier = pltpu.get_barrier_semaphore()
    for peer in exchange.peers:
        pl.semaphore_signal(barrier, inc=1, device_id={"tp": peer})
    return lambda: pl.semaphore_wait(barrier, exchange.n - 1)


def layer0_kernel(n, pos_hbm, freq_hbm, x_in, gain_hbm, wq_hbm, wk_hbm, wv_hbm, wo_hbm, k_hbm, v_hbm, wg_hbm, wu_hbm, wd_hbm, kg_hbm,
                  x_out, new_out, k_pre, kl_keep, vl_keep, wo_next, wg, wu, pos_ref, freq_ref, x_ref, gain_ref, xbuf, ebuf, part1, part2, acc_g, acc_u,
                  load_sem, send1, recv1, send2, recv2):
    me = lax.axis_index("tp")
    batch, width = x_in.shape
    window = k_hbm.shape[1]
    q_cols = wq_hbm.shape[2]
    heads = q_cols // HEAD
    half = width // 2
    first_ex, second_ex = Exchange(n, me, part1, send1, recv1), Exchange(n, me, part2, send2, recv2)
    loads = Loads(load_sem)
    small = [loads.add(x_in, x_ref), loads.add(gain_hbm.at[0], gain_ref), loads.add(pos_hbm, pos_ref), loads.add(freq_hbm, freq_ref)]
    qkv = []
    step = width // QKV_CHUNKS
    for h in range(QKV_CHUNKS):
        rows = pl.ds(h * step, step)
        qkv.append([loads.add(wk_hbm.at[0, rows, :], wu.at[rows, pl.ds(q_cols, HEAD)]),
                    loads.add(wv_hbm.at[0, rows, :], wu.at[rows, pl.ds(q_cols + HEAD, HEAD)]),
                    loads.add(wq_hbm.at[0, rows, :], wu.at[rows, pl.ds(0, q_cols)])])
    k_copy, v_copy = loads.add(k_hbm, kl_keep), loads.add(v_hbm, vl_keep)
    wo_copy, wo_again = loads.add(wo_hbm.at[0], wo_next), loads.add(wo_hbm.at[1], wo_next)
    gate, up = row_loads(loads, wg_hbm, 0, wg), row_loads(loads, wu_hbm, 0, wu)
    ff, col_len = wg.shape[1], width // COL_CHUNKS
    places = [(buf, row, col * col_len) for buf, row in ((wg, 0), (wg, ff), (wu, 0)) for col in range(3)][0:COL_CHUNKS]
    down = [loads.add(wd_hbm.at[0, :, pl.ds(i * col_len, col_len)], buf.at[pl.ds(row, ff), pl.ds(col, col_len)]) for i, (buf, row, col) in enumerate(places)]
    down_dots = [(down[i:i + count], *places[i], count * col_len) for i, count in ((0, 3), (3, 3), (6, 1), (7, 1))]
    k_len = kg_hbm.shape[1] // K_PIECES
    k_loads = [loads.add(kg_hbm.at[:, pl.ds(i * k_len, k_len), :], k_pre.at[:, pl.ds(i * k_len, k_len), :]) for i in range(K_PIECES)]
    start_all(small + sum(qkv, []) + [k_copy, v_copy, wo_copy] + gate)
    met = greet(first_ex)

    wait_all(small)
    xbuf[...] = jnp.zeros_like(xbuf)
    xbuf[0:batch, :] = x_ref[...].astype(F32)
    normed = norm_rows(xbuf[...], gain_ref[0:1, :])
    tables = rope_tables(pos_ref, freq_ref, batch)
    joint = jnp.zeros((8, q_cols + 2 * HEAD), F32)
    for h in range(QKV_CHUNKS):
        wait_all(qkv[h])
        span = slice(h * step, (h + 1) * step)
        joint = joint + matmul(normed[:, span], wu[span, 0:q_cols + 2 * HEAD])
    start_all(up)
    key_new = rotate(joint[:, q_cols:q_cols + HEAD], *tables).astype(BF16)
    value_new = joint[:, q_cols + HEAD:q_cols + 2 * HEAD].astype(BF16)
    new_out[0] = key_new
    new_out[1] = value_new
    stacked, lhs = stack_queries(joint[:, 0:q_cols], tables, heads, batch)
    new_weights = capped_exp(jnp.sum(stacked * per_head(key_new, heads), axis=-1, keepdims=True))

    rows = 4 * heads
    block = window // LOCAL_BLOCKS
    slots = row_values([pos_ref[b] % window for b in range(batch)], rows, block)
    col_ids = lax.broadcasted_iota(jnp.int32, (rows, block), 1)

    def score_step(i, total):
        span = pl.ds(pl.multiple_of(i * block, block), block)
        keys = jnp.concatenate([kl_keep[b, span, :] for b in range(batch)], axis=1)
        weights = capped_exp(score_rows(lhs, keys))
        weights = jnp.where(col_ids + i * block == slots, 0.0, weights)
        ebuf[i] = weights
        return total + jnp.sum(weights, axis=-1, keepdims=True)

    def value_step(i, acc):
        span = pl.ds(pl.multiple_of(i * block, block), block)
        values = jnp.concatenate([vl_keep[b, span, :] for b in range(batch)], axis=1)
        return acc + matmul((ebuf[i] * inv_total).astype(BF16), values)

    k_copy.wait()
    inv_total = 1.0 / lax.fori_loop(0, LOCAL_BLOCKS, score_step, new_weights)
    v_copy.wait()
    mixed = lax.fori_loop(0, LOCAL_BLOCKS, value_step, jnp.zeros((rows, batch * HEAD), F32))
    new_probs = (new_weights * inv_total).astype(BF16).astype(F32)
    merged = merge_heads(pick_rows(mixed, heads, batch) + new_probs * per_head(value_new, heads), heads)

    met()
    wo_copy.wait()
    for h in range(2):
        part1[me, :, h * half:(h + 1) * half] = matmul(merged, wo_next[:, h * half:(h + 1) * half]).astype(BF16)
        first_ex.send(h * half, (h + 1) * half)
    start_all(k_loads[:K_EARLY])
    hidden = x_ref[...].astype(F32)
    order = ((0, 0), (0, 1), (1, 0), (1, 1))
    after = {(0, 1): down[:6], (1, 0): down[6:] + k_loads[K_EARLY:] + [wo_again]}
    x_out[...] = mlp_tail(first_ex.summed(batch), hidden, gain_ref, gate, up, order, after, down_dots, wg, wu, acc_g, acc_u, second_ex)
    first_ex.drain()
    second_ex.drain()
    wait_all(k_loads + [wo_again])


def layer0_call(n, positions, freqs, hidden, gains, w_query, w_key, w_value, w_out, k_local, v_local, w_gate, w_up, w_down, k_global):
    batch, width = hidden.shape
    ff = w_gate.shape[2]
    hbm = pl.BlockSpec(memory_space=pl.ANY)
    vmem = pl.BlockSpec(memory_space=pltpu.VMEM)
    args = (positions, freqs, hidden, gains, w_query, w_key, w_value, w_out, k_local, v_local, w_gate, w_up, w_down, k_global)
    return pl.pallas_call(
        functools.partial(layer0_kernel, n),
        name="layer0",
        out_shape=(pltpu.VMEM((batch, width), BF16), pltpu.VMEM((2, 8, HEAD), BF16), pltpu.VMEM(k_global.shape, BF16),
                   pltpu.VMEM(k_local.shape, BF16), pltpu.VMEM(v_local.shape, BF16), pltpu.VMEM(w_out.shape[1:], BF16)),
        in_specs=[hbm] * len(args),
        out_specs=(vmem,) * 6,
        scratch_shapes=[
            pltpu.VMEM((width, ff), BF16),
            pltpu.VMEM((width, ff), BF16),
            pltpu.SMEM((batch,), jnp.int32),
            pltpu.VMEM((1, HEAD), F32),
            pltpu.VMEM((batch, width), BF16),
            pltpu.VMEM((4, width), F32),
            pltpu.VMEM((8, width), F32),
            pltpu.VMEM((LOCAL_BLOCKS, 4 * w_query.shape[2] // HEAD, k_local.shape[1] // LOCAL_BLOCKS), F32),
            pltpu.VMEM((n, 4, width), BF16),
            pltpu.VMEM((n, 4, width), BF16),
            pltpu.VMEM((8, ff), F32),
            pltpu.VMEM((8, ff), F32),
            pltpu.SemaphoreType.DMA((8 + 3 * QKV_CHUNKS + 2 * ROW_CHUNKS + COL_CHUNKS + K_PIECES,)),
            pltpu.SemaphoreType.DMA((2, n - 1)),
            pltpu.SemaphoreType.DMA((2, n - 1)),
            pltpu.SemaphoreType.DMA((COL_DOTS, n - 1)),
            pltpu.SemaphoreType.DMA((COL_DOTS, n - 1)),
        ],
        compiler_params=pltpu.CompilerParams(vmem_limit_bytes=LAYER0_MIB * MIB, collective_id=0, has_side_effects=True),
    )(*(in_hbm(value) for value in args))


def attn_kernel(layer, block, window, pos_hbm, freq_hbm, x_ref, new_ref, gain_hbm, wq_hbm, wk_hbm, wv_hbm, wo, kbuf, v_hbm, klbuf, vlbuf,
                o_ref, k_out, v_out, kl_out, vl_out, vbuf, wq, wk, wv, pos_ref, freq_ref, gain_ref, xbuf, ebuf, tiles,
                load_sem, t_sem, kout_sem, vout_sem, loc_sem):
    batch, length = v_hbm.shape[0], v_hbm.shape[1]
    heads = wq.shape[1] // HEAD
    blocks = length // block

    def piece(i):
        return pl.ds(pl.multiple_of(i * block, block), block)

    def v_load(i):
        return COPY(v_hbm.at[:, piece(i), :], vbuf.at[:, piece(i), :], load_sem.at[6 + i])

    def k_back(i):
        return COPY(kbuf.at[:, piece(i), :], k_out.at[:, piece(i), :], kout_sem.at[i])

    def v_back(i):
        return COPY(vbuf.at[:, piece(i), :], v_out.at[:, piece(i), :], vout_sem.at[i])

    loads = Loads(load_sem)
    gain_copy, pos_copy, freq_copy = loads.add(gain_hbm.at[layer], gain_ref), loads.add(pos_hbm, pos_ref), loads.add(freq_hbm, freq_ref)
    wk_copy, wq_copy, wv_copy = loads.add(wk_hbm.at[layer], wk), loads.add(wq_hbm.at[layer], wq), loads.add(wv_hbm.at[layer], wv)
    start_all([gain_copy, pos_copy, freq_copy, wk_copy, wq_copy, wv_copy])
    for i in range(blocks):
        v_load(i).start()
    loc_back = [COPY(klbuf, kl_out, loc_sem.at[0]), COPY(vlbuf, vl_out, loc_sem.at[1])]

    xbuf[...] = jnp.zeros_like(xbuf)
    gain_copy.wait()
    xbuf[0:batch, :] = x_ref[...].astype(F32)
    normed = norm_rows(xbuf[...], gain_ref[0:1, :])
    pos_copy.wait()
    freq_copy.wait()
    tables = rope_tables(pos_ref, freq_ref, batch)
    wk_copy.wait()
    key_new = rotate(matmul(normed, wk[...]), *tables).astype(BF16)
    wq_copy.wait()
    queries = matmul(normed, wq[...])
    stacked, lhs = stack_queries(queries, tables, heads, batch)
    wv_copy.wait()
    for i in range(blocks):
        k_back(i).start()
    start_all(loc_back)
    value_new = matmul(normed, wv[...]).astype(BF16)
    new_weights = capped_exp(jnp.sum(stacked * per_head(key_new, heads), axis=-1, keepdims=True))
    rows = 4 * heads
    tile_rows = lax.broadcasted_iota(jnp.int32, (16, HEAD), 0)

    def with_row(buf, new_rows, b, slot):
        base = pl.multiple_of((slot // 16) * 16, 16)
        tile = buf[b, pl.ds(base, 16), :].astype(F32)
        new_row = jnp.broadcast_to(new_rows[b:b + 1, :].astype(F32), (16, HEAD))
        return base, jnp.where(tile_rows == slot - base, new_row, tile).astype(BF16)

    col_ids = lax.broadcasted_iota(jnp.int32, (rows, block), 1)
    limits = row_values([pos_ref[b] for b in range(batch)], rows, block)

    def score_step(i, total):
        keys = jnp.concatenate([kbuf[b, piece(i), :] for b in range(batch)], axis=1)
        weights = capped_exp(score_rows(lhs, keys))
        col_pos = col_ids + i * block
        weights = jnp.where(col_pos < limits, weights, jnp.where(col_pos == limits, new_weights, 0.0))
        ebuf[i] = weights
        return total + jnp.sum(weights, axis=-1, keepdims=True)

    total = lax.fori_loop(0, blocks, score_step, jnp.zeros((rows, 1), F32))
    inv_total = 1.0 / total

    def value_step(i, acc):
        v_load(i).wait()
        for b in range(batch):
            @pl.when(pos_ref[b] // block == i)
            def _():
                base, tile = with_row(vbuf, value_new, b, pos_ref[b])
                vbuf[b, pl.ds(base, 16), :] = tile
        values = jnp.concatenate([vbuf[b, piece(i), :] for b in range(batch)], axis=1)
        out = acc + matmul((ebuf[i] * inv_total).astype(BF16), values)
        v_back(i).start()
        return out

    mixed = lax.fori_loop(0, blocks, value_step, jnp.zeros((rows, batch * HEAD), F32))
    merged = merge_heads(pick_rows(mixed, heads, batch), heads)
    for i in range(blocks):
        k_back(i).wait()
    wait_all(loc_back)
    tile_copies = []
    for which, (buf, out, new_rows) in enumerate(((kbuf, k_out, key_new), (klbuf, kl_out, new_ref[0]), (vlbuf, vl_out, new_ref[1]))):
        for b in range(batch):
            i = which * batch + b
            base, tiles[i] = with_row(buf, new_rows, b, pos_ref[b] % window if which else pos_ref[b])
            tile_copies.append(COPY(tiles.at[i], out.at[b, pl.ds(base, 16), :], t_sem.at[i]))
    o_ref[...] = matmul(merged, wo[...]).astype(BF16)
    start_all(tile_copies)
    for i in range(blocks):
        v_back(i).wait()
    wait_all(tile_copies)


def attn_call(layer, block, positions, freqs, hidden, new_rows, gains, w_query, w_key, w_value, w_out, k_pre, v_cache, k_local, v_local):
    batch, length, head = v_cache.shape
    width, q_cols = w_query.shape[1:]
    blocks = length // block
    vmem = pl.BlockSpec(memory_space=pltpu.VMEM)
    hbm = pl.BlockSpec(memory_space=pl.ANY)
    cache = jax.ShapeDtypeStruct(v_cache.shape, BF16)
    local = jax.ShapeDtypeStruct(k_local.shape, BF16)
    return pl.pallas_call(
        functools.partial(attn_kernel, layer, block, k_local.shape[1]),
        name=f"attn{layer}",
        out_shape=(pltpu.VMEM((4, width), BF16), cache, cache, local, local),
        in_specs=[hbm, hbm, vmem, vmem] + [hbm] * 4 + [vmem, vmem, hbm, vmem, vmem],
        out_specs=(vmem, hbm, hbm, hbm, hbm),
        scratch_shapes=[
            pltpu.VMEM(v_cache.shape, BF16),
            pltpu.VMEM((width, q_cols), BF16),
            pltpu.VMEM((width, head), BF16),
            pltpu.VMEM((width, head), BF16),
            pltpu.SMEM((batch,), jnp.int32),
            pltpu.VMEM((1, head), F32),
            pltpu.VMEM((4, width), F32),
            pltpu.VMEM((8, width), F32),
            pltpu.VMEM((blocks, 4 * q_cols // head, block), F32),
            pltpu.VMEM((3 * batch, 16, head), BF16),
            pltpu.SemaphoreType.DMA((6 + blocks,)),
            pltpu.SemaphoreType.DMA((3 * batch,)),
            pltpu.SemaphoreType.DMA((blocks,)),
            pltpu.SemaphoreType.DMA((blocks,)),
            pltpu.SemaphoreType.DMA((2,)),
        ],
        compiler_params=pltpu.CompilerParams(vmem_limit_bytes=ATTN_MIB * MIB),
    )(in_hbm(positions), in_hbm(freqs), in_vmem(hidden), in_vmem(new_rows), *(in_hbm(value) for value in (gains, w_query, w_key, w_value)),
      in_vmem(w_out), in_vmem(k_pre), in_hbm(v_cache), in_vmem(k_local), in_vmem(v_local))


def mlp_kernel(layer, n, o_ref, x_ref, gain_hbm, wg_hbm, wu_hbm, wd_hbm, x_out, wg, wu, wd, gain_ref, part1, part2, acc_g, acc_u,
               load_sem, send1, recv1, send2, recv2):
    me = lax.axis_index("tp")
    batch, width = x_ref.shape
    first_ex, second_ex = Exchange(n, me, part1, send1, recv1), Exchange(n, me, part2, send2, recv2)
    loads = Loads(load_sem)
    gain_copy = loads.add(gain_hbm.at[layer], gain_ref)
    gate, up = row_loads(loads, wg_hbm, layer, wg), row_loads(loads, wu_hbm, layer, wu)
    col_len = width // COL_CHUNKS
    down = [loads.add(wd_hbm.at[layer, :, pl.ds(i * col_len, col_len)], wd.at[:, pl.ds(i * col_len, col_len)]) for i in range(COL_CHUNKS)]
    down_dots = [(down[i:i + count], wd, 0, i * col_len, count * col_len) for i, count in ((0, 3), (3, 3), (6, 1), (7, 1))]
    part = ROW_CHUNKS // ROW_DOTS
    ordered = [gain_copy]
    for d in range(ROW_DOTS):
        ordered += gate[d * part:(d + 1) * part] + up[d * part:(d + 1) * part]
    start_all(ordered + down)
    met = greet(first_ex)
    part1[me] = o_ref[...]
    met()
    for h in range(2):
        first_ex.send(h * width // 2, (h + 1) * width // 2)
    gain_copy.wait()
    order = tuple((kind, d) for d in range(ROW_DOTS) for kind in range(2))
    x_out[...] = mlp_tail(first_ex.summed(batch), x_ref[...].astype(F32), gain_ref, gate, up, order, {}, down_dots, wg, wu, acc_g, acc_u, second_ex)
    first_ex.drain()
    second_ex.drain()


def mlp_call(layer, n, o_part, hidden, gains, w_gate, w_up, w_down):
    batch, width = hidden.shape
    ff = w_gate.shape[2]
    vmem = pl.BlockSpec(memory_space=pltpu.VMEM)
    hbm = pl.BlockSpec(memory_space=pl.ANY)
    return pl.pallas_call(
        functools.partial(mlp_kernel, layer, n),
        name=f"mlp{layer}",
        out_shape=jax.ShapeDtypeStruct((batch, width), BF16),
        in_specs=[vmem, vmem] + [hbm] * 4,
        out_specs=vmem,
        scratch_shapes=[
            pltpu.VMEM((width, ff), BF16),
            pltpu.VMEM((width, ff), BF16),
            pltpu.VMEM((ff, width), BF16),
            pltpu.VMEM((4, width), F32),
            pltpu.VMEM((n, 4, width), BF16),
            pltpu.VMEM((n, 4, width), BF16),
            pltpu.VMEM((8, ff), F32),
            pltpu.VMEM((8, ff), F32),
            pltpu.SemaphoreType.DMA((1 + 2 * ROW_CHUNKS + COL_CHUNKS,)),
            pltpu.SemaphoreType.DMA((2, n - 1)),
            pltpu.SemaphoreType.DMA((2, n - 1)),
            pltpu.SemaphoreType.DMA((COL_DOTS, n - 1)),
            pltpu.SemaphoreType.DMA((COL_DOTS, n - 1)),
        ],
        compiler_params=pltpu.CompilerParams(vmem_limit_bytes=44 * MIB + MIB // 2, collective_id=layer, has_side_effects=True),
    )(in_vmem(o_part), in_vmem(hidden), *(in_hbm(value) for value in (gains, w_gate, w_up, w_down)))


def decode_step(n, hidden, positions, k_local, v_local, k_global, v_global, w_query, w_key, w_value, w_out, w_gate, w_up, w_down, norm_scale):
    freqs = np.float32(ROPE_BASE) ** (np.float32(-2.0) * np.arange(HEAD // 2, dtype=np.float32) / np.float32(HEAD))
    freqs = jnp.asarray(np.concatenate([freqs, freqs])[None, :])
    k_loc, v_loc, k_glo, v_glo = (cache.reshape(cache.shape[0], cache.shape[1], HEAD) for cache in (k_local, v_local, k_global, v_global))
    heads = (norm_scale, w_query, w_key, w_value, w_out)
    hidden, new_rows, k_pre, k_loc, v_loc, w_next = layer0_call(n, positions, freqs, hidden, *heads, k_loc, v_loc, w_gate, w_up, w_down, k_glo)
    o_part, k_glo, v_glo, k_loc, v_loc = attn_call(1, 4096, positions, freqs, hidden, new_rows, *heads[:4], w_next, k_pre, v_glo, k_loc, v_loc)
    hidden = mlp_call(1, n, o_part, hidden, norm_scale, w_gate, w_up, w_down)
    return (hidden, k_loc.reshape(k_local.shape), v_loc.reshape(v_local.shape), k_glo.reshape(k_global.shape), v_glo.reshape(v_global.shape))


def solution(mesh):
    row_spec = P('dp', None)
    cache_spec = P('dp', None, 'tp', None)
    col_split = P(None, None, 'tp')
    row_split = P(None, 'tp', None)
    in_specs = (row_spec, P('dp'), cache_spec, cache_spec, cache_spec, cache_spec, col_split, col_split, col_split, row_split, col_split, col_split, row_split, P())
    out_specs = (row_spec, cache_spec, cache_spec, cache_spec, cache_spec)
    body = functools.partial(decode_step, mesh.shape['tp'])
    return jax.shard_map(body, mesh=mesh, in_specs=in_specs, out_specs=out_specs, check_vma=False)
```

time: 236 us -> 71.2 us (0.30)
  blocking collectives: 95.9 us -> 0 us
  matrix products: 72.1 us -> 0 us
  Pallas kernels: 0 us -> 69.9 us
  other arithmetic: 49 us -> 0 us
  local copies, waits for them, and re-layouts: 16.7 us -> 0.62 us
    psum x4 -> x0, blocking collectives: 95.9 us -> none  [the longest x2 49.3 us: decoder_layer(): attn_sum = lax.psum(attn_part.astype(jnp.bfloat16), 'tp')]
    pallas_call x0 -> x3, Pallas kernels: none -> 69.9 us  [the longest x1 28.4 us: layer0_call(): pl.pallas_call(functools.partial(layer0_kernel, n), name='layer0', out_sh...]
    dot_general x15 -> x0, matrix products: 69.7 us -> none  [the longest x2 23.4 us: mlp_part(): return jnp.dot(hidden_act, w_down, preferred_element_type=jnp.float32)]
    select_n x2 -> x0, other arithmetic: 40.2 us -> none  [project_and_store(): jnp.where(slot_hit, key_new.astype(jnp.bfloat16)[:, None], k_cache)]
    dot_general x3 -> x0, local copies, waits for them, and re-layouts: 16.6 us -> none  [project_and_store(): jnp.dot(normed, w_query, preferred_element_type=jnp.float32)]
    reduce_sum x9 -> x0, other arithmetic: 2.77 us -> none  [the longest x8 2.15 us: rms_norm(): jnp.mean(values_f32 * values_f32, axis=-1, keepdims=True) + NORM_EPS]
    sub x1 -> x0, matrix products: 2.4 us -> none  [attention(): attn_probs = jax.nn.softmax(logits, axis=-1).astype(jnp.bfloat16)]
where the time goes in v3:
time: 71.2 us; the launch traced here: 71.1 us
  Pallas kernels  69.9 us (98%)
    pallas_call x1, Pallas kernels, layer0_call(): pl.pallas_call(functools.partial(layer0_kernel, n), name='layer0', out_sh...  28.4 us
    pallas_call x1, Pallas kernels, attn_call(): pl.pallas_call(functools.partial(attn_kernel, layer, block, k_local.shape...  21.9 us
    pallas_call x1, Pallas kernels, mlp_call(): pl.pallas_call(functools.partial(mlp_kernel, layer, n), name=f'mlp{layer}...  19.5 us

profile of v3, /device:TPU:0, one launch (start us, length us, event | category | flops | bytes accessed | tf_op | source)
XLA Modules:
  0.0 71.1 jit_solution(9123536575731683610)
XLA Ops:
  0.6 28.4 %layer0.1 = (bf16[3,4096]{1,0:T(4,128)(2,1)S(1)}, bf16[2,8,128]{2,1,0:T(8,128)(2,1)S(1)}, bf16[3,24576,128]{2,1,0:T(8,128)(2,1)S(1)}, bf16[3,4096,128]{2,1,0:T(8...) custom-call(s32[3]{0:T(128)} %pos_hbm.3, f32[1,128]{1,0:T(1,128)} %constant.2.clone.freq_hbm, ...), custom_call_target="tpu_custom_call" | custom-call | tf_op jit(solution)/shard_map/layer0/pallas_call | solution.py:286
  29.1 21.9 %attn1.1 = (bf16[4,4096]{1,0:T(4,128)(2,1)S(1)}, bf16[3,24576,128]{2,1,0:T(8,128)(2,1)}, bf16[3,24576,128]{2,1,0:T(8,128)(2,1)}, bf16[3,4096,128]{2,1,0:T(8,128)(2,1)}, bf16[3,4096,128]{2,1,0:T(8,128)(2,1)}) custom-call(s32[3]{0:T(128)} %pos_hbm.3, f32[1,128]{1,0:T(1,128)} %constant.2.clone.freq_hbm, bf16[3,4096]{1,0:T(4,128)(2,1)S(1)} %get-tuple-element.16.x_ref, ...), custom_call_target="tpu_custom_call" | custom-call | tf_op jit(solution)/shard_map/attn1/pallas_call | solution.py:422
  51.0 19.5 %mlp1.1 = bf16[3,4096]{1,0:T(4,128)(2,1)S(1)} custom-call(bf16[4,4096]{1,0:T(4,128)(2,1)S(1)} %get-tuple-element.22.o_ref, bf16[3,4096]{1,0:T(4,128)(2,1)S(1)} %get-tuple-element.16.x_ref, f32[2,4,4096]{2,1,0:T(4,128)} %gain_hbm.5, bf16[2,4096,1792]{2,1,0:T(8,128)(2,1)} %wg_hbm.3, bf16[2,4096,1792]{2,1,0:T(8,128)(2,1)} %wu_hbm.3, bf16[2,1792,4096]{2,1,0:T(8,128)(2,1)} %wd_hbm.3), custom_call_target="tpu_custom_call" | custom-call | tf_op jit(solution)/shard_map/mlp1/pallas_call | solution.py:483
  70.5 0.6 copy.25

commit v4 on v3

--- a/solution.py
+++ b/solution.py
@@ -15,10 +15,12 @@
 MIB = 1024 * 1024
 F32 = jnp.float32
 BF16 = jnp.bfloat16
-ROW_CHUNKS, ROW_DOTS = 8, 2
+ROW_CHUNKS, ROW_DOTS = 2, 2
 COL_CHUNKS, COL_DOTS = 8, 4
-K_EARLY = 4
-K_PIECES = 12
+GROUPS = ((0, 3), (3, 3), (6, 1), (7, 1))
+K_EARLY = 2
+TAIL_GROUPS = ((0, 6), (6, 5), (11, 3), (14, 2))
+K_PIECES = 6
 LOCAL_BLOCKS = 2
 LAYER0_MIB, ATTN_MIB = 32, 32
 QKV_CHUNKS = 4
@@ -200,23 +202,20 @@
     first_ex, second_ex = Exchange(n, me, part1, send1, recv1), Exchange(n, me, part2, send2, recv2)
     loads = Loads(load_sem)
     small = [loads.add(x_in, x_ref), loads.add(gain_hbm.at[0], gain_ref), loads.add(pos_hbm, pos_ref), loads.add(freq_hbm, freq_ref)]
-    qkv = []
+    wk_copy, wv_copy = loads.add(wk_hbm.at[0], wu.at[:, pl.ds(q_cols, HEAD)]), loads.add(wv_hbm.at[0], wu.at[:, pl.ds(q_cols + HEAD, HEAD)])
     step = width // QKV_CHUNKS
-    for h in range(QKV_CHUNKS):
-        rows = pl.ds(h * step, step)
-        qkv.append([loads.add(wk_hbm.at[0, rows, :], wu.at[rows, pl.ds(q_cols, HEAD)]),
-                    loads.add(wv_hbm.at[0, rows, :], wu.at[rows, pl.ds(q_cols + HEAD, HEAD)]),
-                    loads.add(wq_hbm.at[0, rows, :], wu.at[rows, pl.ds(0, q_cols)])])
+    qkv = [loads.add(wq_hbm.at[0, pl.ds(h * step, step), :], wu.at[pl.ds(h * step, step), pl.ds(0, q_cols)]) for h in range(QKV_CHUNKS)]
     k_copy, v_copy = loads.add(k_hbm, kl_keep), loads.add(v_hbm, vl_keep)
     wo_copy, wo_again = loads.add(wo_hbm.at[0], wo_next), loads.add(wo_hbm.at[1], wo_next)
     gate, up = row_loads(loads, wg_hbm, 0, wg), row_loads(loads, wu_hbm, 0, wu)
     ff, col_len = wg.shape[1], width // COL_CHUNKS
     places = [(buf, row, col * col_len) for buf, row in ((wg, 0), (wg, ff), (wu, 0)) for col in range(3)][0:COL_CHUNKS]
-    down = [loads.add(wd_hbm.at[0, :, pl.ds(i * col_len, col_len)], buf.at[pl.ds(row, ff), pl.ds(col, col_len)]) for i, (buf, row, col) in enumerate(places)]
-    down_dots = [(down[i:i + count], *places[i], count * col_len) for i, count in ((0, 3), (3, 3), (6, 1), (7, 1))]
+    down = [loads.add(wd_hbm.at[0, :, pl.ds(i * col_len, count * col_len)], places[i][0].at[pl.ds(places[i][1], ff), pl.ds(places[i][2], count * col_len)])
+            for i, count in GROUPS]
+    down_dots = [([load], *places[i], count * col_len) for load, (i, count) in zip(down, GROUPS)]
     k_len = kg_hbm.shape[1] // K_PIECES
     k_loads = [loads.add(kg_hbm.at[:, pl.ds(i * k_len, k_len), :], k_pre.at[:, pl.ds(i * k_len, k_len), :]) for i in range(K_PIECES)]
-    start_all(small + sum(qkv, []) + [k_copy, v_copy, wo_copy] + gate)
+    start_all(small + [wk_copy, wv_copy] + qkv + [k_copy, v_copy, wo_copy] + gate)
     met = greet(first_ex)
 
     wait_all(small)
@@ -225,8 +224,9 @@
     normed = norm_rows(xbuf[...], gain_ref[0:1, :])
     tables = rope_tables(pos_ref, freq_ref, batch)
     joint = jnp.zeros((8, q_cols + 2 * HEAD), F32)
+    wait_all([wk_copy, wv_copy])
     for h in range(QKV_CHUNKS):
-        wait_all(qkv[h])
+        qkv[h].wait()
         span = slice(h * step, (h + 1) * step)
         joint = joint + matmul(normed[:, span], wu[span, 0:q_cols + 2 * HEAD])
     start_all(up)
@@ -270,7 +270,7 @@
     start_all(k_loads[:K_EARLY])
     hidden = x_ref[...].astype(F32)
     order = ((0, 0), (0, 1), (1, 0), (1, 1))
-    after = {(0, 1): down[:6], (1, 0): down[6:] + k_loads[K_EARLY:] + [wo_again]}
+    after = {(0, 1): down[:2], (1, 0): down[2:] + k_loads[K_EARLY:] + [wo_again]}
     x_out[...] = mlp_tail(first_ex.summed(batch), hidden, gain_ref, gate, up, order, after, down_dots, wg, wu, acc_g, acc_u, second_ex)
     first_ex.drain()
     second_ex.drain()
@@ -353,9 +353,6 @@
     queries = matmul(normed, wq[...])
     stacked, lhs = stack_queries(queries, tables, heads, batch)
     wv_copy.wait()
-    for i in range(blocks):
-        k_back(i).start()
-    start_all(loc_back)
     value_new = matmul(normed, wv[...]).astype(BF16)
     new_weights = capped_exp(jnp.sum(stacked * per_head(key_new, heads), axis=-1, keepdims=True))
     rows = 4 * heads
@@ -371,6 +368,12 @@
     limits = row_values([pos_ref[b] for b in range(batch)], rows, block)
 
     def score_step(i, total):
+        @pl.when(i == 3)
+        def _():
+            for j in range(blocks):
+                k_back(j).start()
+            start_all(loc_back)
+
         keys = jnp.concatenate([kbuf[b, piece(i), :] for b in range(batch)], axis=1)
         weights = capped_exp(score_rows(lhs, keys))
         col_pos = col_ids + i * block
@@ -455,9 +458,9 @@
     loads = Loads(load_sem)
     gain_copy = loads.add(gain_hbm.at[layer], gain_ref)
     gate, up = row_loads(loads, wg_hbm, layer, wg), row_loads(loads, wu_hbm, layer, wu)
-    col_len = width // COL_CHUNKS
-    down = [loads.add(wd_hbm.at[layer, :, pl.ds(i * col_len, col_len)], wd.at[:, pl.ds(i * col_len, col_len)]) for i in range(COL_CHUNKS)]
-    down_dots = [(down[i:i + count], wd, 0, i * col_len, count * col_len) for i, count in ((0, 3), (3, 3), (6, 1), (7, 1))]
+    col_len = width // 16
+    down = [loads.add(wd_hbm.at[layer, :, pl.ds(i * col_len, count * col_len)], wd.at[:, pl.ds(i * col_len, count * col_len)]) for i, count in TAIL_GROUPS]
+    down_dots = [([load], wd, 0, i * col_len, count * col_len) for load, (i, count) in zip(down, TAIL_GROUPS)]
     part = ROW_CHUNKS // ROW_DOTS
     ordered = [gain_copy]
     for d in range(ROW_DOTS):
@@ -498,8 +501,8 @@
             pltpu.SemaphoreType.DMA((1 + 2 * ROW_CHUNKS + COL_CHUNKS,)),
             pltpu.SemaphoreType.DMA((2, n - 1)),
             pltpu.SemaphoreType.DMA((2, n - 1)),
-            pltpu.SemaphoreType.DMA((COL_DOTS, n - 1)),
-            pltpu.SemaphoreType.DMA((COL_DOTS, n - 1)),
+            pltpu.SemaphoreType.DMA((4, n - 1)),
+            pltpu.SemaphoreType.DMA((4, n - 1)),
         ],
         compiler_params=pltpu.CompilerParams(vmem_limit_bytes=44 * MIB + MIB // 2, collective_id=layer, has_side_effects=True),
     )(in_vmem(o_part), in_vmem(hidden), *(in_hbm(value) for value in (gains, w_gate, w_up, w_down)))

time: 71.2 us -> 70.1 us (0.985)
  Pallas kernels: 69.9 us -> 68.7 us
    pallas_call x1, Pallas kernels: 21.9 us -> 21.2 us  [attn_call(): pl.pallas_call(functools.partial(attn_kernel, layer, block, k_local.shape...]
where the time goes in v4:
time: 70.1 us; the launch traced here: 70 us
  Pallas kernels  68.7 us (98%)
    pallas_call x1, Pallas kernels, layer0_call(): pl.pallas_call(functools.partial(layer0_kernel, n), name='layer0', out_sh...  28.2 us
    pallas_call x1, Pallas kernels, attn_call(): pl.pallas_call(functools.partial(attn_kernel, layer, block, k_local.shape...  21.2 us
    pallas_call x1, Pallas kernels, mlp_call(): pl.pallas_call(functools.partial(mlp_kernel, layer, n), name=f'mlp{layer}...  19.3 us

profile of v4, /device:TPU:0, one launch (start us, length us, event | category | flops | bytes accessed | tf_op | source)
XLA Modules:
  0.0 70.0 jit_solution(2742261436916100321)
XLA Ops:
  0.6 28.2 %layer0.1 = (bf16[3,4096]{1,0:T(4,128)(2,1)S(1)}, bf16[2,8,128]{2,1,0:T(8,128)(2,1)S(1)}, bf16[3,24576,128]{2,1,0:T(8,128)(2,1)S(1)}, bf16[3,4096,128]{2,1,0:T(8...) custom-call(s32[3]{0:T(128)} %pos_hbm.3, f32[1,128]{1,0:T(1,128)} %constant.2.clone.freq_hbm, ...), custom_call_target="tpu_custom_call" | custom-call | tf_op jit(solution)/shard_map/layer0/pallas_call | solution.py:286
  28.9 21.2 %attn1.1 = (bf16[4,4096]{1,0:T(4,128)(2,1)S(1)}, bf16[3,24576,128]{2,1,0:T(8,128)(2,1)}, bf16[3,24576,128]{2,1,0:T(8,128)(2,1)}, bf16[3,4096,128]{2,1,0:T(8,128)(2,1)}, bf16[3,4096,128]{2,1,0:T(8,128)(2,1)}) custom-call(s32[3]{0:T(128)} %pos_hbm.3, f32[1,128]{1,0:T(1,128)} %constant.2.clone.freq_hbm, bf16[3,4096]{1,0:T(4,128)(2,1)S(1)} %get-tuple-element.16.x_ref, ...), custom_call_target="tpu_custom_call" | custom-call | tf_op jit(solution)/shard_map/attn1/pallas_call | solution.py:425
  50.1 19.3 %mlp1.1 = bf16[3,4096]{1,0:T(4,128)(2,1)S(1)} custom-call(bf16[4,4096]{1,0:T(4,128)(2,1)S(1)} %get-tuple-element.22.o_ref, bf16[3,4096]{1,0:T(4,128)(2,1)S(1)} %get-tuple-element.16.x_ref, f32[2,4,4096]{2,1,0:T(4,128)} %gain_hbm.5, bf16[2,4096,1792]{2,1,0:T(8,128)(2,1)} %wg_hbm.3, bf16[2,4096,1792]{2,1,0:T(8,128)(2,1)} %wu_hbm.3, bf16[2,1792,4096]{2,1,0:T(8,128)(2,1)} %wd_hbm.3), custom_call_target="tpu_custom_call" | custom-call | tf_op jit(solution)/shard_map/mlp1/pallas_call | solution.py:486
  69.4 0.6 copy.25

commit v5 on v4

--- a/solution.py
+++ b/solution.py
@@ -136,16 +136,19 @@
             group[k].start()
         self.sent.append((group, first, last))
 
-    def summed(self, batch):
-        parts = []
+    def summed_norm(self, batch, gain_row):
+        parts, squares, gain = [], [], 1.0 + gain_row
         for group, first, last in self.sent:
             for copy in group:
                 copy.wait_recv()
             acc = self.buf[0, :, first:last].astype(F32)
             for j in range(1, self.n):
                 acc = acc + self.buf[j, :, first:last].astype(F32)
+            acc = acc[0:batch]
             parts.append(acc)
-        return jnp.concatenate(parts, axis=1)[0:batch]
+            squares.append(jnp.sum(acc * acc, axis=-1, keepdims=True))
+        inv_rms = lax.rsqrt(sum(squares) / self.buf.shape[2] + NORM_EPS)
+        return jnp.concatenate([(part * inv_rms * gain[:, first:last]).astype(BF16) for part, (_, first, last) in zip(parts, self.sent)], axis=1)
 
     def drain(self):
         for group, _, _ in self.sent:
@@ -160,7 +163,7 @@
 
 def mlp_tail(branch, hidden, gain_ref, gate, up, order, after, down_dots, wg, wu, acc_g, acc_u, exchange):
     batch, width = hidden.shape
-    mid = (hidden + norm_rows(branch, gain_ref[1:2, :]).astype(F32)).astype(BF16).astype(F32)
+    mid = (hidden + branch.astype(F32)).astype(BF16).astype(F32)
     pre = norm_rows(mid, gain_ref[2:3, :])
     part = ROW_CHUNKS // ROW_DOTS
     row_len = width // ROW_DOTS
@@ -179,8 +182,7 @@
         exchange.buf[exchange.me, 0:batch, first:last] = matmul(act, buf[row:row + act.shape[1], col:col + cols]).astype(BF16)
         exchange.send(first, last)
         first = last
-    total = exchange.summed(batch)
-    return (mid + norm_rows(total, gain_ref[3:4, :]).astype(F32)).astype(BF16)
+    return (mid + exchange.summed_norm(batch, gain_ref[3:4, :]).astype(F32)).astype(BF16)
 
 
 def greet(exchange):
@@ -270,8 +272,8 @@
     start_all(k_loads[:K_EARLY])
     hidden = x_ref[...].astype(F32)
     order = ((0, 0), (0, 1), (1, 0), (1, 1))
-    after = {(0, 1): down[:2], (1, 0): down[2:] + k_loads[K_EARLY:] + [wo_again]}
-    x_out[...] = mlp_tail(first_ex.summed(batch), hidden, gain_ref, gate, up, order, after, down_dots, wg, wu, acc_g, acc_u, second_ex)
+    after = {(0, 0): down[:1], (0, 1): down[1:2], (1, 0): down[2:] + k_loads[K_EARLY:] + [wo_again]}
+    x_out[...] = mlp_tail(first_ex.summed_norm(batch, gain_ref[1:2, :]), hidden, gain_ref, gate, up, order, after, down_dots, wg, wu, acc_g, acc_u, second_ex)
     first_ex.drain()
     second_ex.drain()
     wait_all(k_loads + [wo_again])
@@ -473,7 +475,7 @@
         first_ex.send(h * width // 2, (h + 1) * width // 2)
     gain_copy.wait()
     order = tuple((kind, d) for d in range(ROW_DOTS) for kind in range(2))
-    x_out[...] = mlp_tail(first_ex.summed(batch), x_ref[...].astype(F32), gain_ref, gate, up, order, {}, down_dots, wg, wu, acc_g, acc_u, second_ex)
+    x_out[...] = mlp_tail(first_ex.summed_norm(batch, gain_ref[1:2, :]), x_ref[...].astype(F32), gain_ref, gate, up, order, {}, down_dots, wg, wu, acc_g, acc_u, second_ex)
     first_ex.drain()
     second_ex.drain()
 

time: 70.1 us -> 70.1 us (level)
  no operation moved by 1% of the time
where the time goes in v5:
time: 70.1 us; the launch traced here: 70 us
  Pallas kernels  68.7 us (98%)
    pallas_call x1, Pallas kernels, layer0_call(): pl.pallas_call(functools.partial(layer0_kernel, n), name='layer0', out_sh...  28.2 us
    pallas_call x1, Pallas kernels, attn_call(): pl.pallas_call(functools.partial(attn_kernel, layer, block, k_local.shape...  21.2 us
    pallas_call x1, Pallas kernels, mlp_call(): pl.pallas_call(functools.partial(mlp_kernel, layer, n), name=f'mlp{layer}...  19.3 us

profile of v5, /device:TPU:0, one launch (start us, length us, event | category | flops | bytes accessed | tf_op | source)
XLA Modules:
  0.0 70.0 jit_solution(14204507508389981605)
XLA Ops:
  0.6 28.2 %layer0.1 = (bf16[3,4096]{1,0:T(4,128)(2,1)S(1)}, bf16[2,8,128]{2,1,0:T(8,128)(2,1)S(1)}, bf16[3,24576,128]{2,1,0:T(8,128)(2,1)S(1)}, bf16[3,4096,128]{2,1,0:T(8...) custom-call(s32[3]{0:T(128)} %pos_hbm.3, f32[1,128]{1,0:T(1,128)} %constant.2.clone.freq_hbm, ...), custom_call_target="tpu_custom_call" | custom-call | tf_op jit(solution)/shard_map/layer0/pallas_call | solution.py:288
  28.9 21.2 %attn1.1 = (bf16[4,4096]{1,0:T(4,128)(2,1)S(1)}, bf16[3,24576,128]{2,1,0:T(8,128)(2,1)}, bf16[3,24576,128]{2,1,0:T(8,128)(2,1)}, bf16[3,4096,128]{2,1,0:T(8,128)(2,1)}, bf16[3,4096,128]{2,1,0:T(8,128)(2,1)}) custom-call(s32[3]{0:T(128)} %pos_hbm.3, f32[1,128]{1,0:T(1,128)} %constant.2.clone.freq_hbm, bf16[3,4096]{1,0:T(4,128)(2,1)S(1)} %get-tuple-element.16.x_ref, ...), custom_call_target="tpu_custom_call" | custom-call | tf_op jit(solution)/shard_map/attn1/pallas_call | solution.py:427
  50.0 19.3 %mlp1.1 = bf16[3,4096]{1,0:T(4,128)(2,1)S(1)} custom-call(bf16[4,4096]{1,0:T(4,128)(2,1)S(1)} %get-tuple-element.22.o_ref, bf16[3,4096]{1,0:T(4,128)(2,1)S(1)} %get-tuple-element.16.x_ref, f32[2,4,4096]{2,1,0:T(4,128)} %gain_hbm.5, bf16[2,4096,1792]{2,1,0:T(8,128)(2,1)} %wg_hbm.3, bf16[2,4096,1792]{2,1,0:T(8,128)(2,1)} %wu_hbm.3, bf16[2,1792,4096]{2,1,0:T(8,128)(2,1)} %wd_hbm.3), custom_call_target="tpu_custom_call" | custom-call | tf_op jit(solution)/shard_map/mlp1/pallas_call | solution.py:488
  69.3 0.6 copy.25
